TPU v7x, 128 devices: a whole 4x4x4 slice. The times are simulated.
128 devices in a mesh: seq: 8 (over y_lo, x), tp: 8 (over z, core), grp: 2 (over y_hi).
Axes of the slice: x: 4, y: 4 (y_hi: 2, y_lo: 2; y = y_hi * 2 + y_lo), z: 4, core: 2. Of those that a mesh axis runs over, the one named last changes fastest.
Arguments:
- query: bfloat16 [16, 64, 8192], P('grp', None, 'tp'), parts along dimension 0, may hold values from -15 to 15
- cache: bfloat16 [16, 16384, 8, 256], P('grp', 'tp', 'seq'), parts along dimension 0, may hold values from -6 to 6
- head_of_slot: int32 [16], P('grp'), parts along dimension 0, may hold values from 0 to 7, each once
- lengths: int32 [16], P('grp'), parts along dimension 0, may hold values from 8192 to 16384
- out_weight: bfloat16 [8192, 8192], P('tp', 'seq'), may hold values from -0.0625 to 0.0625
Outputs:
- projected: bfloat16 [16, 64, 8192], P(('grp', 'tp'), None, 'seq'), parts along dimension 0
There are 2 independent parts, one for each index of `grp`. A program takes and returns all parts, laid end to end along the dimension named above; an argument that names none is the same for every part. Nothing has to cross between parts.
Inputs may be any that keep to these rules, and one draw needn't show every extreme that they name: head_of_slot names every KV head exactly once.
All inputs are finite; a program needn't handle non-finite values.
Results may differ from a plain program's by a relative error of at most 0.01.
Values may be sent and summed in bfloat16 or wider, within the bound.
No kernel may reach another device: no remote copies, remote signals or barrier semaphores. Data moves between devices by JAX's collectives and lax.ppermute only.
A program may use at most 128 MiB of HBM per device.

v0:
```python
import functools
import math

import jax
import jax.numpy as jnp
from jax import lax
from jax.experimental import pallas as pl
from jax.experimental.pallas import tpu as pltpu
from jax.sharding import PartitionSpec as P


HD = 128
MASKED = -1e30
LOG2E = math.log2(math.e)
EXTRA = 128
CHUNKS = 2


def split3(x):
    hi = x.astype(jnp.bfloat16)
    rest = x - hi.astype(jnp.float32)
    mid = rest.astype(jnp.bfloat16)
    low = (rest - mid.astype(jnp.float32)).astype(jnp.bfloat16)
    return hi, mid, low


def joined(ext):
    return ext + (pltpu.roll(ext, EXTRA - 8, 1) + pltpu.roll(ext, EXTRA - 16, 1))


def packed(lse):
    lane = lax.broadcasted_iota(jnp.int32, lse.shape, 1)
    hi, mid, low = (part.astype(jnp.float32) for part in split3(lse))
    out = jnp.where(lane < 8, hi, 0.0)
    out = jnp.where((lane >= 8) & (lane < 16), pltpu.roll(mid, 8, 1), out)
    out = jnp.where((lane >= 16) & (lane < 24), pltpu.roll(low, 16, 1), out)
    return out.astype(jnp.bfloat16)


def attention_body(lengths, *refs, block, group, place):
    *q_refs, kv_ref, sent_ref, kept_ref = refs
    step = pl.program_id(0)
    count = sent_ref.shape[1] - 1
    tokens = q_refs[0].shape[1]
    chunk = q_refs[0].shape[0]
    extent = kv_ref.shape[1]
    rank = lax.axis_index("tp")
    core = rank % 2
    seq = place(core, step)
    first = rank * extent
    length = lengths[seq]
    c2 = LOG2E / math.sqrt(HD)
    lane = lax.broadcasted_iota(jnp.int32, (tokens, EXTRA), 1)

    def put(target, source, normal, lse):
        hi, mid, low = (part.astype(jnp.float32) for part in split3(lse))
        target[source, step] = normal
        old = target[source, count].astype(jnp.float32)
        old = jnp.where(step == 0, 0.0, old)
        old = jnp.where(lane == seq, hi, old)
        old = jnp.where(lane == seq + 8, mid, old)
        target[source, count] = jnp.where(lane == seq + 16, low, old).astype(jnp.bfloat16)

    def emit(normals, lses):
        for source in range(group // 2):
            pair = [(normals[2 * source + p], lses[2 * source + p]) for p in range(2)]
            picked = [jnp.where(core == 0, a, b) for a, b in zip(*pair)]
            other = [jnp.where(core == 0, b, a) for a, b in zip(*pair)]
            put(kept_ref, source, *picked)
            put(sent_ref, source, *other)

    def compute(masked):
        whole = q_refs[0][step % chunk]
        for n in range(1, len(q_refs)):
            whole = jnp.where(step >= n * chunk, q_refs[n][step % chunk], whole)
        q = jnp.concatenate([whole[:, HD * h : HD * (h + 1)] for h in range(group)], axis=0)

        def scored(at):
            return lax.dot_general(
                q,
                kv_ref[0, at : at + block, :HD],
                (((1,), (1,)), ((), ())),
                preferred_element_type=jnp.float32,
            )

        top = None
        upcoming = scored(0)
        for at in range(0, extent, block):
            scores = upcoming
            if at + block < extent:
                upcoming = scored(at + block)
            if masked:
                pos = first + at + lax.broadcasted_iota(jnp.int32, (tokens, block), 1)
                limit = length - tokens + lax.broadcasted_iota(jnp.int32, (tokens, block), 0)
                visible = jnp.concatenate([pos <= limit] * group, axis=0)
                scores = jnp.where(visible, scores, MASKED)
            here = jnp.max(scores, axis=1, keepdims=True)
            new_top = here if top is None else jnp.maximum(top, here)
            weights = jnp.exp2((scores - new_top) * c2)
            if masked:
                weights = jnp.where(visible, weights, 0.0)
            values = kv_ref[0, at : at + block, HD:]
            both = jnp.concatenate([values, jnp.ones_like(values)], axis=1)
            sums = jnp.dot(weights.astype(jnp.bfloat16), both, preferred_element_type=jnp.float32)
            part, part_total = sums[:, :HD], sums[:, HD:]
            if top is None:
                blended, totals = part, part_total
            else:
                shrink = jnp.exp2((top - new_top) * c2)
                blended = blended * shrink + part
                totals = totals * shrink + part_total
            top = new_top
        if masked:
            totals = jnp.where(totals > 0.0, totals, 1.0)
        normal = (blended / totals).astype(jnp.bfloat16)
        lse = top * c2 + jnp.log2(totals)
        cuts = [slice(tokens * h, tokens * (h + 1)) for h in range(group)]
        emit([normal[cut] for cut in cuts], [lse[cut] for cut in cuts])

    full = first + extent - 1 <= length - tokens
    hidden = first > length - 1

    @pl.when(full)
    def _():
        compute(False)

    @pl.when(jnp.logical_not(full | hidden))
    def _():
        compute(True)

    @pl.when(hidden)
    def _():
        zero = jnp.zeros((tokens, HD), jnp.bfloat16)
        nothing = jnp.full((tokens, EXTRA), MASKED, jnp.float32)
        emit([zero] * group, [nothing] * group)


def attention(lengths, parts, kv, group, place):
    chunk, tokens, _ = parts[0].shape
    count = chunk * len(parts)
    extent = kv.shape[1]
    shape = (group // 2, count + 1, tokens, HD)
    whole = pl.BlockSpec(memory_space=pltpu.VMEM)
    block_of = lambda i, m: (place(lax.axis_index("tp") % 2, i), 0, 0)
    return pl.pallas_call(
        functools.partial(attention_body, block=512, group=group, place=place),
        grid_spec=pltpu.PrefetchScalarGridSpec(
            num_scalar_prefetch=1,
            grid=(count,),
            in_specs=[whole] * len(parts) + [pl.BlockSpec((1, extent, 2 * HD), block_of)],
            out_specs=[whole, whole],
        ),
        out_shape=[jax.ShapeDtypeStruct(shape, jnp.bfloat16)] * 2,
        compiler_params=pltpu.CompilerParams(vmem_limit_bytes=50 * 1024 * 1024),
        cost_estimate=pl.CostEstimate(
            flops=count * tokens * group * extent * HD * 4,
            bytes_accessed=count * extent * 2 * HD * 2,
            transcendentals=count * tokens * group * extent,
        ),
        name="attend",
    )(lengths, *parts, kv)


def pack_rows_body(own_ref, other_ref, *outs):
    z = lax.axis_index("tp") // 2
    for r, out_ref in enumerate(outs):
        out_ref[0] = own_ref[z ^ (r + 1)]
        out_ref[1] = other_ref[z ^ (r + 1)]


def pack_rows(own, other):
    shape = jax.ShapeDtypeStruct((2,) + own.shape[1:], own.dtype)
    return small_call(pack_rows_body, [own, other], [shape] * (own.shape[0] - 1), 5_000_000)


def split_rows_body(w_ref, own_ref, other_ref):
    core = lax.axis_index("tp") % 2
    for v in range(w_ref.shape[0]):
        own_ref[v] = w_ref[v, core]
        other_ref[v] = w_ref[v, 1 - core]


def split_rows(w):
    shape = jax.ShapeDtypeStruct((w.shape[0],) + w.shape[2:], w.dtype)
    return small_call(split_rows_body, [w], [shape, shape], 5_000_000)


def cut_query_body(q_ref, *refs, chunks):
    *outs, sems = refs
    core = lax.axis_index("tp") % 2
    count = outs[0].shape[0]
    half = count * chunks
    copies = []
    for n, half_of in enumerate((core, 1 - core)):
        for k in range(chunks):
            source = q_ref.at[pl.ds(half_of * half + k * count, count)]
            copies.append(pltpu.make_async_copy(source, outs[n * chunks + k], sems.at[n, k]))
    for copy in copies:
        copy.start()
    for copy in copies:
        copy.wait()


def cut_query(query, chunks):
    shape = jax.ShapeDtypeStruct((query.shape[0] // (2 * chunks),) + query.shape[1:], query.dtype)
    return pl.pallas_call(
        functools.partial(cut_query_body, chunks=chunks),
        in_specs=[pl.BlockSpec(memory_space=pltpu.HBM)],
        out_specs=[pl.BlockSpec(memory_space=pltpu.VMEM)] * (2 * chunks),
        out_shape=[shape] * (2 * chunks),
        scratch_shapes=[pltpu.SemaphoreType.DMA((2, chunks))],
        compiler_params=pltpu.CompilerParams(vmem_limit_bytes=24 * 1024 * 1024),
        cost_estimate=pl.CostEstimate(flops=1_000_000, bytes_accessed=4 * query.size, transcendentals=0),
        name="cut_query",
    )(query)


def choose_body(head_of_slot, a_ref, b_ref, out_ref, *, first):
    rank = lax.axis_index("tp")
    head = head_of_slot[lax.axis_index("seq")]
    take_first = first(rank % 2, rank // 2, head)

    @pl.when(take_first)
    def _():
        out_ref[...] = a_ref[...]

    @pl.when(jnp.logical_not(take_first))
    def _():
        out_ref[...] = b_ref[...]


def choose(head_of_slot, a, b, first):
    shape = jax.ShapeDtypeStruct(a.shape, a.dtype)
    body = functools.partial(choose_body, first=first)
    return small_call(body, [a, b], [shape], 1_000_000, prefetch=(head_of_slot,))[0]


def merge_shares(parts):
    top = functools.reduce(jnp.maximum, parts)
    weights = [jnp.exp2(part - top) for part in parts]
    total = functools.reduce(jnp.add, weights)
    return [w / total for w in weights], top + jnp.log2(total)


def small_call(body, operands, out_shape, flops, prefetch=(), scratch=()):
    whole = pl.BlockSpec(memory_space=pltpu.VMEM)

    return pl.pallas_call(
        body,
        grid_spec=pltpu.PrefetchScalarGridSpec(
            num_scalar_prefetch=len(prefetch),
            grid=(1,),
            in_specs=[whole] * len(operands),
            out_specs=[whole] * len(out_shape),
            scratch_shapes=list(scratch),
        ),
        out_shape=out_shape,
        compiler_params=pltpu.CompilerParams(vmem_limit_bytes=24 * 1024 * 1024),
        cost_estimate=pl.CostEstimate(flops=flops, bytes_accessed=2_000_000, transcendentals=0),
    )(*prefetch, *operands)


def merge_pair_body(*refs, groups, chips):
    *refs, out_ref = refs
    core = lax.axis_index("tp") % 2
    tokens = out_ref.shape[2]
    seqs = out_ref.shape[1] - 1
    half_len = seqs // 2
    lane = lax.broadcasted_iota(jnp.int32, (tokens, EXTRA), 1)
    for chip in range(chips):
        ext = [joined(ref[chip, ref.shape[1] - 1].astype(jnp.float32)) for ref in refs]
        joint = jnp.zeros((tokens, EXTRA), jnp.float32)
        for a, a_at, b, b_at, own_half, offset, count in groups:
            shares, lse = merge_shares([ext[a], ext[b]])
            half = core if own_half else 1 - core
            start = half * half_len + offset
            joint = jnp.where((lane >= start) & (lane < start + count), lse, joint)
            share = jnp.where(half == 0, shares[0], pltpu.roll(shares[0], EXTRA - half_len, 1))
            for i in range(count):
                kept = refs[a][chip, a_at + i].astype(jnp.float32)
                came = refs[b][chip, b_at + i].astype(jnp.float32)
                out_ref[chip, start + i] = (
                    came + (kept - came) * share[:, offset + i : offset + i + 1]
                ).astype(jnp.bfloat16)
        out_ref[chip, seqs] = packed(joint)


def merge_pair(parts, groups, seqs):
    chips, _, tokens, _ = parts[0].shape
    return small_call(
        functools.partial(merge_pair_body, groups=groups, chips=chips),
        parts,
        [jax.ShapeDtypeStruct((chips, seqs + 1, tokens, HD), jnp.bfloat16)],
        40_000_000,
    )[0]


def merge_all_body(x_ref, out_ref):
    count, seqs = x_ref.shape[0], out_ref.shape[0]
    shares, _ = merge_shares([joined(x_ref[k, seqs].astype(jnp.float32)) for k in range(count)])
    for b in range(seqs):
        parts = [x_ref[k, b].astype(jnp.float32) * shares[k][:, b : b + 1] for k in range(count)]
        out_ref[b] = functools.reduce(jnp.add, parts).astype(jnp.bfloat16)


def merge_all(x):
    _, seqs, tokens, width = x.shape
    return small_call(
        merge_all_body, [x], [jax.ShapeDtypeStruct((seqs - 1, tokens, width), jnp.bfloat16)], 20_000_000
    )[0]


def project_body(head_of_slot, *refs, count, own_parity):
    pieces = refs[:count]
    own_ref, came_ref, flip_ref, far_ref, far_hop_ref, mirror_ref, out_ref, w_ref = refs[count:]
    tokens = pieces[0].shape[2]
    half = pieces[0].shape[0]
    seq_rank = lax.axis_index("seq")
    rank = lax.axis_index("tp")
    core, z = rank % 2, rank // 2
    parity = core if own_parity else 1 - core
    w_ref[0, 0] = own_ref[z]
    w_ref[0, 1] = came_ref[z]
    w_ref[1] = flip_ref[...]
    w_ref[half - 1] = mirror_ref[...]

    @pl.when(core == 0)
    def _():
        w_ref[2] = far_ref[...]

    @pl.when(core == 1)
    def _():
        w_ref[2] = far_hop_ref[...]

    x = jnp.concatenate([ref[:, parity].reshape(half * tokens, HD) for ref in pieces], axis=1)
    rows = []
    for k in range(count):
        head = head_of_slot[seq_rank ^ k]
        rows.append(w_ref[(head // 2) ^ z, (head % 2) ^ core])
    y = jnp.dot(x, jnp.concatenate(rows, axis=0), preferred_element_type=jnp.float32)
    out_ref[...] = y.reshape(out_ref.shape).astype(out_ref.dtype)


def project(head_of_slot, pieces, blocks, own_parity, dtype):
    count = len(pieces)
    half, _, tokens, _ = pieces[0].shape
    width = blocks[0].shape[-1]
    return small_call(
        functools.partial(project_body, count=count, own_parity=own_parity),
        [*pieces, *blocks],
        [jax.ShapeDtypeStruct((half, tokens, width), dtype)],
        2 * half * tokens * count * HD * width,
        prefetch=(head_of_slot,),
        scratch=[pltpu.VMEM((half, 2, HD, width), jnp.bfloat16)],
    )[0]


def layer(query, cache, head_of_slot, lengths, out_weight):
    seqs, tokens, width = query.shape
    group = width // HD
    half = seqs // 2
    tp_size = lax.axis_size("tp")
    chips = tp_size // 2
    seq_size = lax.axis_size("seq")
    kv = cache.reshape(seqs, cache.shape[1], cache.shape[3])

    def send(x, axis, pairs):
        return lax.ppermute(x, axis, pairs)

    ring = range(chips)
    swap_core = [(i, i ^ 1) for i in range(tp_size)]
    to_flip = [(2 * v + c, 2 * (v ^ 1) + c) for v in ring for c in range(2)]
    to_mirror = [(2 * v + c, 2 * (chips - 1 - v) + c) for v in ring for c in range(2)]
    first_hop = to_flip[0::2] + to_mirror[1::2]
    second_hop = to_mirror[0::2] + to_flip[1::2]

    def partner(core, z):
        return jnp.where(core == 0, z ^ 1, chips - 1 - z)

    def owned(core, z, head):
        return head % 2 == core

    def unreached(core, z, head):
        return partner(core, z) != head // 2

    def reached(core, z, head):
        return (z == head // 2) | (partner(core, z) == head // 2)

    chunk = half // CHUNKS
    cuts = cut_query(query, CHUNKS)
    came = [send(cuts[n], "tp", swap_core) for n in range(CHUNKS)]
    parts = [choose(head_of_slot, cuts[CHUNKS + n], new, owned) for n, new in enumerate(came)]
    came = [send(part, "tp", first_hop) for part in parts]
    parts = [choose(head_of_slot, part, new, unreached) for new, part in zip(came, parts)]
    came = [send(part, "tp", second_hop) for part in parts]
    parts = [choose(head_of_slot, part, new, reached) for new, part in zip(came, parts)]
    rest = [send(part, "tp", swap_core) for part in parts]
    own, other = split_rows(out_weight.reshape(chips, 2, HD, out_weight.shape[1]))
    swapped = send(other, "tp", swap_core)
    for_flip, for_far, for_mirror = pack_rows(own, swapped)
    flipped = send(for_flip, "tp", to_flip)
    mirrored = send(for_mirror, "tp", to_mirror)
    down = [(2 * v + 1, 2 * ((v - 1) % chips) + 1) for v in ring]
    far = send(for_far, "tp", [(2 * v, 2 * (v ^ 2)) for v in ring] + down)
    far_hop = send(far, "tp", down)
    blocks = [own, swapped, flipped, far, far_hop, mirrored]

    left = half - chunk

    def later(core, step):
        own_half = (1 - core) * half + chunk + step
        return jnp.where(step < left, own_half, core * half + step - left)

    first = attention(lengths, parts[:1], kv, group, lambda core, step: (1 - core) * half + step)
    first_came = send(first[0], "tp", swap_core)
    second = attention(lengths, parts[1:] + rest, kv, group, later)
    second_came = send(second[0], "tp", swap_core)
    groups = (
        (2, left, 1, 0, True, 0, chunk),
        (2, half, 3, 0, True, chunk, left),
        (0, 0, 3, left, False, 0, chunk),
        (2, 0, 3, half, False, chunk, left),
    )
    by_chip = merge_pair([first[1], first_came, second[1], second_came], groups, seqs)
    z_groups = [[2 * v + c for v in ring] for c in range(2)]

    def spread(x):
        return lax.all_to_all(x, "tp", 0, 0, tiled=True, axis_index_groups=z_groups)

    piece = merge_all(spread(by_chip))

    pieces = [piece] + [send(piece, "seq", [(i, i ^ k) for i in range(seq_size)]) for k in range(1, seq_size)]
    pieces = [p.reshape(chips, 2, tokens, HD) for p in pieces]
    sent = project(head_of_slot, pieces, blocks, False, jnp.bfloat16)
    came = send(sent, "tp", swap_core)
    kept = project(head_of_slot, pieces, blocks, True, jnp.float32)
    sums = (kept + came.astype(jnp.float32)).astype(jnp.bfloat16)
    arrived = spread(sums)
    return jnp.sum(arrived.astype(jnp.float32), axis=0, keepdims=True).astype(jnp.bfloat16)


def solution(mesh):
    in_specs = (
        P("grp", None, "tp"),
        P("grp", "tp", "seq", None),
        P("grp"),
        P("grp"),
        P("tp", "seq"),
    )
    out_specs = P(("grp", "tp"), None, "seq")
    return jax.shard_map(layer, mesh=mesh, in_specs=in_specs, out_specs=out_specs, check_vma=False)
```

profile of v0, /device:TPU:1, one launch (start us, length us, event | category | flops | bytes accessed | tf_op | source)
XLA Modules:
  0.0 113.8 jit_solution(5195376520139616377)
XLA Ops:
  0.0 1.2 %copy-done.1 = bf16[8,64,1024]{2,1,0:T(8,128)(2,1)S(1)} copy-done((bf16[8,64,1024]{2,1,0:T(8,128)(2,1)S(1)}, bf16[8,64,1024]{2,1,0:T(8,128)(2,1)}, u32[]{:S(2)}) %copy-start.1) | copy-done | bytes 1048600
  1.3 1.5 %collective-permute-start = (bf16[2,64,1024]{2,1,0:T(8,128)(2,1)S(1)}, bf16[2,64,1024]{2,1,0:T(8,128)(2,1)S(1)}, u32[]{:S(2)}, u32[]{:S(2)}) collective-permute-start(bf16[2,64,1024]{2,1,0:T(8,128)(2,1)S(1)} %get-tuple-element.19), channel_id=1, source_target_pairs={{0,2},{2,0},{4,6},{6,4},{8,10},{10,8},{12,14},{14,12},{1,3},{3,1},... | collective-permute-start | bytes 786440 | tf_op jit(solution)/shard_map/ppermute | solution.py:368
  2.9 1.1 collective-permute-done.b_ref
  4.0 0.7 copy-done.2
  4.6 0.6 shard_map.55.a_ref
  5.2 3.9 %collective-permute-start.1 = (bf16[2,64,1024]{2,1,0:T(8,128)(2,1)S(1)}, bf16[2,64,1024]{2,1,0:T(8,128)(2,1)S(1)}, u32[]{:S(2)}, u32[]{:S(2)}) collective-permute-start(bf16[2,64,1024]{2,1,0:T(8,128)(2,1)S(1)} %shard_map.55.a_ref), channel_id=1, source_target_pairs={{0,4},{4,0},{8,12},{12,8},{2,14},{6,10},{10,6},{14,2},{1,5},{5,1},... | collective-permute-start | bytes 786440 | tf_op jit(solution)/shard_map/ppermute | solution.py:368
  9.2 0.6 shard_map.58.a_ref
  9.9 1.6 %copy-done = bf16[1024,1024]{1,0:T(8,128)(2,1)S(1)} copy-done((bf16[1024,1024]{1,0:T(8,128)(2,1)S(1)}, bf16[1024,1024]{1,0:T(8,128)(2,1)}, u32[]{:S(2)}) %copy-start) | copy-done | bytes 2097176
  11.7 1.2 %collective-permute-done.1.b_ref = bf16[2,64,1024]{2,1,0:T(8,128)(2,1)S(1)} collective-permute-done((bf16[2,64,1024]{2,1,0:T(8,128)(2,1)S(1)}, bf16[2,64,1024]{2,1,0:T(8,128)(2,1)S(1)}, u32[]{:S(2)}, u32[]{:S(2)}) %collective-permute-start.1) | collective-permute-done | bytes 262176 | tf_op jit(solution)/shard_map/ppermute | solution.py:368
  12.9 0.7 copy-done.3
  13.6 0.6 shard_map.56.a_ref
  14.3 2.0 %collective-permute-done.5.b_ref = bf16[2,64,1024]{2,1,0:T(8,128)(2,1)S(1)} collective-permute-done((bf16[2,64,1024]{2,1,0:T(8,128)(2,1)S(1)}, bf16[2,64,1024]{2,1,0:T(8,128)(2,1)S(1)}, u32[]{:S(2)}, u32[]{:S(2)}) %collective-permute-start.5) | collective-permute-done | bytes 262176 | tf_op jit(solution)/shard_map/ppermute | solution.py:368
  16.3 0.6 shard_map.59.a_ref
  17.0 2.8 %collective-permute-done.2.b_ref = bf16[2,64,1024]{2,1,0:T(8,128)(2,1)S(1)} collective-permute-done((bf16[2,64,1024]{2,1,0:T(8,128)(2,1)S(1)}, bf16[2,64,1024]{2,1,0:T(8,128)(2,1)S(1)}, u32[]{:S(2)}, u32[]{:S(2)}) %collective-permute-start.2) | collective-permute-done | bytes 262176 | tf_op jit(solution)/shard_map/ppermute | solution.py:368
  19.8 0.6 shard_map.57.refs_0_
  20.4 2.2 %collective-permute-start.7 = (bf16[2,64,1024]{2,1,0:T(8,128)(2,1)S(1)}, bf16[2,64,1024]{2,1,0:T(8,128)(2,1)S(1)}, u32[]{:S(2)}, u32[]{:S(2)}) collective-permute-start(bf16[2,64,1024]{2,1,0:T(8,128)(2,1)S(1)} %shard_map.57.refs_0_), channel_id=1, source_target_pairs={{0,2},{2,0},{4,6},{6,4},{8,10},{10,8},{12,14},{14,12},{1,3},{3,1},... | collective-permute-start | bytes 786440 | tf_op jit(solution)/shard_map/ppermute | solution.py:368
  22.6 0.6 shard_map.60.refs_0_
  23.2 3.3 %collective-permute-start.8 = (bf16[2,64,1024]{2,1,0:T(8,128)(2,1)S(1)}, bf16[2,64,1024]{2,1,0:T(8,128)(2,1)S(1)}, u32[]{:S(2)}, u32[]{:S(2)}) collective-permute-start(bf16[2,64,1024]{2,1,0:T(8,128)(2,1)S(1)} %shard_map.60.refs_0_), channel_id=1, source_target_pairs={{0,2},{2,0},{4,6},{6,4},{8,10},{10,8},{12,14},{14,12},{1,3},{3,1},... | collective-permute-start | bytes 786440 | tf_op jit(solution)/shard_map/ppermute | solution.py:368
  26.5 1.2 %collective-permute-done.8.refs_2_ = bf16[2,64,1024]{2,1,0:T(8,128)(2,1)S(1)} collective-permute-done((bf16[2,64,1024]{2,1,0:T(8,128)(2,1)S(1)}, bf16[2,64,1024]{2,1,0:T(8,128)(2,1)S(1)}, u32[]{:S(2)}, u32[]{:S(2)}) %collective-permute-start.8) | collective-permute-done | bytes 262176 | tf_op jit(solution)/shard_map/ppermute | solution.py:368
  27.6 0.7 copy-done.5
  28.3 11.7 %attend.3 = (bf16[4,7,64,128]{3,2,1,0:T(8,128)(2,1)S(1)}, bf16[4,7,64,128]{3,2,1,0:T(8,128)(2,1)S(1)}) custom-call(s32[8]{0:T(128)S(1)} %copy-done.5, bf16[2,64,1024]{2,1,0:T(8,128)(2,1)S(1)} %shard_map.60.refs_0_, bf16[2,64,1024]{2,1,0:T(8,128)(2,1)S(1)} %collective-permute-done.7.refs_1_, bf16[2,64,1024]{2,1,0:T(8,128)(2,1)S(1)} %collective-permute-done.8.refs_2_, ...), custom_call_target="tpu_custom_call" | custom-call | flops 3221225472 | bytes 6291456 | tf_op jit(solution)/shard_map/attend/pallas_call | solution.py:145
  40.0 0.5 collective-permute-start.9
  40.4 1.1 shard_map.64
  41.5 5.1 %attend.2 = (bf16[4,3,64,128]{3,2,1,0:T(8,128)(2,1)S(1)}, bf16[4,3,64,128]{3,2,1,0:T(8,128)(2,1)S(1)}) custom-call(s32[8]{0:T(128)S(1)} %copy-done.5, bf16[2,64,1024]{2,1,0:T(8,128)(2,1)S(1)} %shard_map.57.refs_0_, bf16[8,2048,256]{2,1,0:T(8,128)(2,1)} %bitcast.29), custom_call_target="tpu_custom_call" | custom-call | flops 1073741824 | bytes 2097152 | tf_op jit(solution)/shard_map/attend/pallas_call | solution.py:145
  46.6 1.4 %collective-permute-start.3 = (bf16[4,3,64,128]{3,2,1,0:T(8,128)(2,1)S(1)}, bf16[4,3,64,128]{3,2,1,0:T(8,128)(2,1)S(1)}, u32[]{:S(2)}, u32[]{:S(2)}) collective-permute-start(bf16[4,3,64,128]{3,2,1,0:T(8,128)(2,1)S(1)} %get-tuple-element.21), channel_id=1, source_target_pairs={{0,2},{2,0},{4,6},{6,4},{8,10},{10,8},{12,14},{14,12},{1,3},{3,1},... | collective-permute-start | bytes 589832 | tf_op jit(solution)/shard_map/ppermute | solution.py:368
  48.0 0.4 collective-permute-start.18
  48.4 0.6 collective-permute-done.3.refs_1_
  49.1 2.5 %shard_map.61 = bf16[4,9,64,128]{3,2,1,0:T(8,128)(2,1)} custom-call(bf16[4,3,64,128]{3,2,1,0:T(8,128)(2,1)S(1)} %get-tuple-element.20.refs_0_, bf16[4,3,64,128]{3,2,1,0:T(8,128)(2,1)S(1)} %collective-permute-done.3.refs_1_, bf16[4,7,64,128]{3,2,1,0:T(8,128)(2,1)S(1)} %get-tuple-element.24.refs_2_, bf16[4,7,64,128]{3,2,1,0:T(8,128)(2,1)S(1)} %collective-permute-done.9.refs_3_), custom_call_target="tpu_custom_call" | custom-call | flops 40000000 | bytes 2000000 | tf_op jit(solution)/shard_map/pallas_call | solution.py:248
  51.6 3.5 %all-to-all-start = ((bf16[4,9,64,128]{3,2,1,0:T(8,128)(2,1)}), bf16[4,9,64,128]{3,2,1,0:T(8,128)(2,1)S(1)}, u32[]{:S(2)}, u32[]{:S(2)}) async-start(bf16[4,9,64,128]{3,2,1,0:T(8,128)(2,1)} %shard_map.61), calls=%async_computation | async-start | bytes 1179648 | tf_op jit(solution)/shard_map/all_to_all | solution.py:428
  55.1 2.6 %collective-permute-start.21 = (bf16[2,128,1024]{2,1,0:T(8,128)(2,1)}, bf16[2,128,1024]{2,1,0:T(8,128)(2,1)}, u32[]{:S(2)}, u32[]{:S(2)}) collective-permute-start(bf16[2,128,1024]{2,1,0:T(8,128)(2,1)} %copy-done.6), channel_id=1, source_target_pairs={{0,12},{2,14},{4,8},{6,10},{8,4},{10,6},{12,0},{14,2},{1,13},{3,15... | collective-permute-start | bytes 1572872 | tf_op jit(solution)/shard_map/ppermute | solution.py:368
  57.7 2.0 %collective-permute-start.20 = (bf16[2,128,1024]{2,1,0:T(8,128)(2,1)S(1)}, bf16[2,128,1024]{2,1,0:T(8,128)(2,1)}, u32[]{:S(2)}, u32[]{:S(2)}) collective-permute-start(bf16[2,128,1024]{2,1,0:T(8,128)(2,1)S(1)} %collective-permute-done.19.refs_11_), channel_id=1, source_target_pairs={{2,14},{6,2},{10,6},{14,10},{3,15},{7,3},{11,7},{15,11},{18,30},{2... | collective-permute-start | bytes 1572872 | tf_op jit(solution)/shard_map/ppermute | solution.py:368
  59.7 10.4 %all-to-all-done.x_ref = bf16[4,9,64,128]{3,2,1,0:T(8,128)(2,1)S(1)} async-done(((bf16[4,9,64,128]{3,2,1,0:T(8,128)(2,1)}), bf16[4,9,64,128]{3,2,1,0:T(8,128)(2,1)S(1)}, u32[]{:S(2)}, u32[]{:S(2)}) %all-to-all-start) | async-done | bytes 589856 | tf_op jit(solution)/shard_map/all_to_all | solution.py:428
  70.2 0.5 shard_map.62
  70.7 3.6 %collective-permute-start.16 = (bf16[8,64,128]{2,1,0:T(8,128)(2,1)S(1)}, bf16[8,64,128]{2,1,0:T(8,128)(2,1)S(1)}, u32[]{:S(2)}, u32[]{:S(2)}) collective-permute-start(bf16[8,64,128]{2,1,0:T(8,128)(2,1)S(1)} %shard_map.62), channel_id=1, source_target_pairs={{0,112},{16,96},{32,80},{48,64},{64,48},{80,32},{96,16},{112,0},{1... | collective-permute-start | bytes 393224 | tf_op jit(solution)/shard_map/ppermute | solution.py:368
  74.3 0.4 collective-permute-start.15
  74.7 1.3 %collective-permute-start.14 = (bf16[8,64,128]{2,1,0:T(8,128)(2,1)S(1)}, bf16[8,64,128]{2,1,0:T(8,128)(2,1)S(1)}, u32[]{:S(2)}, u32[]{:S(2)}) collective-permute-start(bf16[8,64,128]{2,1,0:T(8,128)(2,1)S(1)} %shard_map.62), channel_id=1, source_target_pairs={{0,80},{16,64},{32,112},{48,96},{64,16},{80,0},{96,48},{112,32},{1... | collective-permute-start | bytes 393224 | tf_op jit(solution)/shard_map/ppermute | solution.py:368
  76.0 1.3 %collective-permute-start.13 = (bf16[8,64,128]{2,1,0:T(8,128)(2,1)S(1)}, bf16[8,64,128]{2,1,0:T(8,128)(2,1)S(1)}, u32[]{:S(2)}, u32[]{:S(2)}) collective-permute-start(bf16[8,64,128]{2,1,0:T(8,128)(2,1)S(1)} %shard_map.62), channel_id=1, source_target_pairs={{0,64},{16,80},{32,96},{48,112},{64,0},{80,16},{96,32},{112,48},{1... | collective-permute-start | bytes 393224 | tf_op jit(solution)/shard_map/ppermute | solution.py:368
  77.3 2.5 %collective-permute-done.16 = bf16[8,64,128]{2,1,0:T(8,128)(2,1)S(1)} collective-permute-done((bf16[8,64,128]{2,1,0:T(8,128)(2,1)S(1)}, bf16[8,64,128]{2,1,0:T(8,128)(2,1)S(1)}, u32[]{:S(2)}, u32[]{:S(2)}) %collective-permute-start.16) | collective-permute-done | bytes 131104 | tf_op jit(solution)/shard_map/ppermute | solution.py:368
  79.8 3.9 %collective-permute-start.12 = (bf16[8,64,128]{2,1,0:T(8,128)(2,1)S(1)}, bf16[8,64,128]{2,1,0:T(8,128)(2,1)S(1)}, u32[]{:S(2)}, u32[]{:S(2)}) collective-permute-start(bf16[8,64,128]{2,1,0:T(8,128)(2,1)S(1)} %shard_map.62), channel_id=1, source_target_pairs={{0,48},{16,32},{32,16},{48,0},{64,112},{80,96},{96,80},{112,64},{1... | collective-permute-start | bytes 393224 | tf_op jit(solution)/shard_map/ppermute | solution.py:368
  83.9 0.3 collective-permute-start.10
  84.3 2.1 %collective-permute-done.13 = bf16[8,64,128]{2,1,0:T(8,128)(2,1)S(1)} collective-permute-done((bf16[8,64,128]{2,1,0:T(8,128)(2,1)S(1)}, bf16[8,64,128]{2,1,0:T(8,128)(2,1)S(1)}, u32[]{:S(2)}, u32[]{:S(2)}) %collective-permute-start.13) | collective-permute-done | bytes 131104 | tf_op jit(solution)/shard_map/ppermute | solution.py:368
  86.4 1.7 %collective-permute-done.12 = bf16[8,64,128]{2,1,0:T(8,128)(2,1)S(1)} collective-permute-done((bf16[8,64,128]{2,1,0:T(8,128)(2,1)S(1)}, bf16[8,64,128]{2,1,0:T(8,128)(2,1)S(1)}, u32[]{:S(2)}, u32[]{:S(2)}) %collective-permute-start.12) | collective-permute-done | bytes 131104 | tf_op jit(solution)/shard_map/ppermute | solution.py:368
  88.1 1.0 collective-permute-done.11
  89.1 2.7 %shard_map.66 = bf16[4,64,1024]{2,1,0:T(8,128)(2,1)S(1)} custom-call(s32[8]{0:T(128)S(1)} %copy-done.4, bf16[4,2,64,128]{3,2,1,0:T(8,128)(2,1)S(1)} %bitcast.12, bf16[4,2,64,128]{3,2,1,0:T(8,128)(2,1)S(1)} %bitcast.26, bf16[4,2,64,128]{3,2,1,0:T(8,128)(2,1)S(1)} %bitcast.24, bf16[4,2,64,128]{3,2,1,0:T(8,128)(2,1)S(1)} %bitcast.22, ...), custom_call_target="tpu_custom_call" | custom-call | flops 536870912 | bytes 2000000 | tf_op jit(solution)/shard_map/pallas_call | solution.py:248
  91.9 3.5 %collective-permute-start.22 = (bf16[4,64,1024]{2,1,0:T(8,128)(2,1)S(1)}, bf16[4,64,1024]{2,1,0:T(8,128)(2,1)S(1)}, u32[]{:S(2)}, u32[]{:S(2)}) collective-permute-start(bf16[4,64,1024]{2,1,0:T(8,128)(2,1)S(1)} %shard_map.66), channel_id=1, source_target_pairs={{0,2},{2,0},{4,6},{6,4},{8,10},{10,8},{12,14},{14,12},{1,3},{3,1},... | collective-permute-start | bytes 1572872 | tf_op jit(solution)/shard_map/ppermute | solution.py:368
  95.4 2.7 %shard_map.65 = f32[4,64,1024]{2,1,0:T(8,128)S(1)} custom-call(s32[8]{0:T(128)S(1)} %copy-done.4, bf16[4,2,64,128]{3,2,1,0:T(8,128)(2,1)S(1)} %bitcast.13, bf16[4,2,64,128]{3,2,1,0:T(8,128)(2,1)S(1)} %bitcast.27, bf16[4,2,64,128]{3,2,1,0:T(8,128)(2,1)S(1)} %bitcast.25, bf16[4,2,64,128]{3,2,1,0:T(8,128)(2,1)S(1)} %bitcast.23, ...), custom_call_target="tpu_custom_call" | custom-call | flops 536870912 | bytes 2000000 | tf_op jit(solution)/shard_map/pallas_call | solution.py:248
  98.3 14.7 %all_to_all.10 = bf16[4,64,1024]{2,1,0:T(8,128)(2,1)S(1)} all-to-all(bf16[4,64,1024]{2,1,0:T(8,128)(2,1)S(1)} %add_convert_fusion), channel_id=1, replica_groups={{0,4,8,12},{2,6,10,14},{1,5,9,13},{3,7,11,15},{16,20,24,28},{18,22,26,3..., dimensions={0} | all-to-all | bytes 1048576 | tf_op jit(solution)/shard_map/all_to_all | solution.py:428
  113.0 0.7 reduce_sum.12
  (32 shorter events, 1.2 us)
Async XLA Ops:
  0.0 1.2 %copy-start.1 = (bf16[8,64,1024]{2,1,0:T(8,128)(2,1)S(1)}, bf16[8,64,1024]{2,1,0:T(8,128)(2,1)}, u32[]{:S(2)}) copy-start(bf16[8,64,1024]{2,1,0:T(8,128)(2,1)} %q_ref.1) | copy-start | bytes 3145732
  1.3 2.6 %collective-permute-start = (bf16[2,64,1024]{2,1,0:T(8,128)(2,1)S(1)}, bf16[2,64,1024]{2,1,0:T(8,128)(2,1)S(1)}, u32[]{:S(2)}, u32[]{:S(2)}) collective-permute-start(bf16[2,64,1024]{2,1,0:T(8,128)(2,1)S(1)} %get-tuple-element.19), channel_id=1, source_target_pairs={{0,2},{2,0},{4,6},{6,4},{8,10},{10,8},{12,14},{14,12},{1,3},{3,1},... | collective-permute-start | bytes 786440 | tf_op jit(solution)/shard_map/ppermute | solution.py:368
  2.8 6.4 %collective-permute-start.4 = (bf16[2,64,1024]{2,1,0:T(8,128)(2,1)S(1)}, bf16[2,64,1024]{2,1,0:T(8,128)(2,1)S(1)}, u32[]{:S(2)}, u32[]{:S(2)}) collective-permute-start(bf16[2,64,1024]{2,1,0:T(8,128)(2,1)S(1)} %get-tuple-element.23), channel_id=1, source_target_pairs={{0,2},{2,0},{4,6},{6,4},{8,10},{10,8},{12,14},{14,12},{1,3},{3,1},... | collective-permute-start | bytes 786440 | tf_op jit(solution)/shard_map/ppermute | solution.py:368
  4.0 0.7 copy-start.2
  5.2 7.7 %collective-permute-start.1 = (bf16[2,64,1024]{2,1,0:T(8,128)(2,1)S(1)}, bf16[2,64,1024]{2,1,0:T(8,128)(2,1)S(1)}, u32[]{:S(2)}, u32[]{:S(2)}) collective-permute-start(bf16[2,64,1024]{2,1,0:T(8,128)(2,1)S(1)} %shard_map.55.a_ref), channel_id=1, source_target_pairs={{0,4},{4,0},{8,12},{12,8},{2,14},{6,10},{10,6},{14,2},{1,5},{5,1},... | collective-permute-start | bytes 786440 | tf_op jit(solution)/shard_map/ppermute | solution.py:368
  9.8 6.5 %collective-permute-start.5 = (bf16[2,64,1024]{2,1,0:T(8,128)(2,1)S(1)}, bf16[2,64,1024]{2,1,0:T(8,128)(2,1)S(1)}, u32[]{:S(2)}, u32[]{:S(2)}) collective-permute-start(bf16[2,64,1024]{2,1,0:T(8,128)(2,1)S(1)} %shard_map.58.a_ref), channel_id=1, source_target_pairs={{0,4},{4,0},{8,12},{12,8},{2,14},{6,10},{10,6},{14,2},{1,5},{5,1},... | collective-permute-start | bytes 786440 | tf_op jit(solution)/shard_map/ppermute | solution.py:368
  9.9 1.6 %copy-start = (bf16[1024,1024]{1,0:T(8,128)(2,1)S(1)}, bf16[1024,1024]{1,0:T(8,128)(2,1)}, u32[]{:S(2)}) copy-start(bf16[1024,1024]{1,0:T(8,128)(2,1)} %param.9) | copy-start | bytes 6291460
  11.6 28.8 %collective-permute-start.17 = (bf16[4,128,1024]{2,1,0:T(8,128)(2,1)S(1)}, bf16[4,128,1024]{2,1,0:T(8,128)(2,1)S(1)}, u32[]{:S(2)}, u32[]{:S(2)}) collective-permute-start(bf16[4,128,1024]{2,1,0:T(8,128)(2,1)S(1)} %get-tuple-element.27), channel_id=1, source_target_pairs={{0,2},{2,0},{4,6},{6,4},{8,10},{10,8},{12,14},{14,12},{1,3},{3,1},... | collective-permute-start | bytes 3145736 | tf_op jit(solution)/shard_map/ppermute | solution.py:368
  12.9 0.7 copy-start.3
  14.2 5.6 %collective-permute-start.2 = (bf16[2,64,1024]{2,1,0:T(8,128)(2,1)S(1)}, bf16[2,64,1024]{2,1,0:T(8,128)(2,1)S(1)}, u32[]{:S(2)}, u32[]{:S(2)}) collective-permute-start(bf16[2,64,1024]{2,1,0:T(8,128)(2,1)S(1)} %shard_map.56.a_ref), channel_id=1, source_target_pairs={{0,12},{4,8},{8,4},{12,0},{2,6},{6,2},{10,14},{14,10},{1,13},{5,9}... | collective-permute-start | bytes 786440 | tf_op jit(solution)/shard_map/ppermute | solution.py:368
  16.9 5.7 %collective-permute-start.6 = (bf16[2,64,1024]{2,1,0:T(8,128)(2,1)S(1)}, bf16[2,64,1024]{2,1,0:T(8,128)(2,1)S(1)}, u32[]{:S(2)}, u32[]{:S(2)}) collective-permute-start(bf16[2,64,1024]{2,1,0:T(8,128)(2,1)S(1)} %shard_map.59.a_ref), channel_id=1, source_target_pairs={{0,12},{4,8},{8,4},{12,0},{2,6},{6,2},{10,14},{14,10},{1,13},{5,9}... | collective-permute-start | bytes 786440 | tf_op jit(solution)/shard_map/ppermute | solution.py:368
  20.4 6.1 %collective-permute-start.7 = (bf16[2,64,1024]{2,1,0:T(8,128)(2,1)S(1)}, bf16[2,64,1024]{2,1,0:T(8,128)(2,1)S(1)}, u32[]{:S(2)}, u32[]{:S(2)}) collective-permute-start(bf16[2,64,1024]{2,1,0:T(8,128)(2,1)S(1)} %shard_map.57.refs_0_), channel_id=1, source_target_pairs={{0,2},{2,0},{4,6},{6,4},{8,10},{10,8},{12,14},{14,12},{1,3},{3,1},... | collective-permute-start | bytes 786440 | tf_op jit(solution)/shard_map/ppermute | solution.py:368
  23.2 4.4 %collective-permute-start.8 = (bf16[2,64,1024]{2,1,0:T(8,128)(2,1)S(1)}, bf16[2,64,1024]{2,1,0:T(8,128)(2,1)S(1)}, u32[]{:S(2)}, u32[]{:S(2)}) collective-permute-start(bf16[2,64,1024]{2,1,0:T(8,128)(2,1)S(1)} %shard_map.60.refs_0_), channel_id=1, source_target_pairs={{0,2},{2,0},{4,6},{6,4},{8,10},{10,8},{12,14},{14,12},{1,3},{3,1},... | collective-permute-start | bytes 786440 | tf_op jit(solution)/shard_map/ppermute | solution.py:368
  27.6 0.7 copy-start.5
  40.0 49.2 %copy-start.4 = (s32[8]{0:T(128)S(1)}, s32[8]{0:T(128)}, u32[]{:S(2)}) copy-start(s32[8]{0:T(128)} %head_of_slot.15) | copy-start | bytes 100
  40.0 9.1 %collective-permute-start.9 = (bf16[4,7,64,128]{3,2,1,0:T(8,128)(2,1)S(1)}, bf16[4,7,64,128]{3,2,1,0:T(8,128)(2,1)S(1)}, u32[]{:S(2)}, u32[]{:S(2)}) collective-permute-start(bf16[4,7,64,128]{3,2,1,0:T(8,128)(2,1)S(1)} %get-tuple-element.25), channel_id=1, source_target_pairs={{0,2},{2,0},{4,6},{6,4},{8,10},{10,8},{12,14},{14,12},{1,3},{3,1},... | collective-permute-start | bytes 1376264 | tf_op jit(solution)/shard_map/ppermute | solution.py:368
  41.5 7.5 %copy-start.6 = (bf16[2,128,1024]{2,1,0:T(8,128)(2,1)}, bf16[2,128,1024]{2,1,0:T(8,128)(2,1)S(1)}, u32[]{:S(2)}) copy-start(bf16[2,128,1024]{2,1,0:T(8,128)(2,1)S(1)} %get-tuple-element.30) | copy-start | bytes 1572868
  41.5 16.2 %collective-permute-start.19 = (bf16[2,128,1024]{2,1,0:T(8,128)(2,1)}, bf16[2,128,1024]{2,1,0:T(8,128)(2,1)S(1)}, u32[]{:S(2)}, u32[]{:S(2)}) collective-permute-start(bf16[2,128,1024]{2,1,0:T(8,128)(2,1)} %get-tuple-element.29), channel_id=1, source_target_pairs={{0,8},{4,12},{8,0},{12,4},{2,14},{6,2},{10,6},{14,10},{1,9},{5,13}... | collective-permute-start | bytes 1572872 | tf_op jit(solution)/shard_map/ppermute | solution.py:368
  46.6 2.4 %collective-permute-start.3 = (bf16[4,3,64,128]{3,2,1,0:T(8,128)(2,1)S(1)}, bf16[4,3,64,128]{3,2,1,0:T(8,128)(2,1)S(1)}, u32[]{:S(2)}, u32[]{:S(2)}) collective-permute-start(bf16[4,3,64,128]{3,2,1,0:T(8,128)(2,1)S(1)} %get-tuple-element.21), channel_id=1, source_target_pairs={{0,2},{2,0},{4,6},{6,4},{8,10},{10,8},{12,14},{14,12},{1,3},{3,1},... | collective-permute-start | bytes 589832 | tf_op jit(solution)/shard_map/ppermute | solution.py:368
  48.0 26.7 %collective-permute-start.18 = (bf16[2,128,1024]{2,1,0:T(8,128)(2,1)}, bf16[2,128,1024]{2,1,0:T(8,128)(2,1)}, u32[]{:S(2)}, u32[]{:S(2)}) collective-permute-start(bf16[2,128,1024]{2,1,0:T(8,128)(2,1)} %get-tuple-element.28), channel_id=1, source_target_pairs={{0,4},{2,6},{4,0},{6,2},{8,12},{10,14},{12,8},{14,10},{1,5},{3,7},... | collective-permute-start | bytes 1572872 | tf_op jit(solution)/shard_map/ppermute | solution.py:368
  51.6 18.6 %all-to-all-start = ((bf16[4,9,64,128]{3,2,1,0:T(8,128)(2,1)}), bf16[4,9,64,128]{3,2,1,0:T(8,128)(2,1)S(1)}, u32[]{:S(2)}, u32[]{:S(2)}) async-start(bf16[4,9,64,128]{3,2,1,0:T(8,128)(2,1)} %shard_map.61), calls=%async_computation | async-start | bytes 1179648 | tf_op jit(solution)/shard_map/all_to_all | solution.py:428
  55.1 20.9 %collective-permute-start.21 = (bf16[2,128,1024]{2,1,0:T(8,128)(2,1)}, bf16[2,128,1024]{2,1,0:T(8,128)(2,1)}, u32[]{:S(2)}, u32[]{:S(2)}) collective-permute-start(bf16[2,128,1024]{2,1,0:T(8,128)(2,1)} %copy-done.6), channel_id=1, source_target_pairs={{0,12},{2,14},{4,8},{6,10},{8,4},{10,6},{12,0},{14,2},{1,13},{3,15... | collective-permute-start | bytes 1572872 | tf_op jit(solution)/shard_map/ppermute | solution.py:368
  57.7 31.4 %collective-permute-start.20 = (bf16[2,128,1024]{2,1,0:T(8,128)(2,1)S(1)}, bf16[2,128,1024]{2,1,0:T(8,128)(2,1)}, u32[]{:S(2)}, u32[]{:S(2)}) collective-permute-start(bf16[2,128,1024]{2,1,0:T(8,128)(2,1)S(1)} %collective-permute-done.19.refs_11_), channel_id=1, source_target_pairs={{2,14},{6,2},{10,6},{14,10},{3,15},{7,3},{11,7},{15,11},{18,30},{2... | collective-permute-start | bytes 1572872 | tf_op jit(solution)/shard_map/ppermute | solution.py:368
  70.7 9.1 %collective-permute-start.16 = (bf16[8,64,128]{2,1,0:T(8,128)(2,1)S(1)}, bf16[8,64,128]{2,1,0:T(8,128)(2,1)S(1)}, u32[]{:S(2)}, u32[]{:S(2)}) collective-permute-start(bf16[8,64,128]{2,1,0:T(8,128)(2,1)S(1)} %shard_map.62), channel_id=1, source_target_pairs={{0,112},{16,96},{32,80},{48,64},{64,48},{80,32},{96,16},{112,0},{1... | collective-permute-start | bytes 393224 | tf_op jit(solution)/shard_map/ppermute | solution.py:368
  74.3 9.4 %collective-permute-start.15 = (bf16[8,64,128]{2,1,0:T(8,128)(2,1)S(1)}, bf16[8,64,128]{2,1,0:T(8,128)(2,1)S(1)}, u32[]{:S(2)}, u32[]{:S(2)}) collective-permute-start(bf16[8,64,128]{2,1,0:T(8,128)(2,1)S(1)} %shard_map.62), channel_id=1, source_target_pairs={{0,96},{16,112},{32,64},{48,80},{64,32},{80,48},{96,0},{112,16},{1... | collective-permute-start | bytes 393224 | tf_op jit(solution)/shard_map/ppermute | solution.py:368
  74.7 9.3 %collective-permute-start.14 = (bf16[8,64,128]{2,1,0:T(8,128)(2,1)S(1)}, bf16[8,64,128]{2,1,0:T(8,128)(2,1)S(1)}, u32[]{:S(2)}, u32[]{:S(2)}) collective-permute-start(bf16[8,64,128]{2,1,0:T(8,128)(2,1)S(1)} %shard_map.62), channel_id=1, source_target_pairs={{0,80},{16,64},{32,112},{48,96},{64,16},{80,0},{96,48},{112,32},{1... | collective-permute-start | bytes 393224 | tf_op jit(solution)/shard_map/ppermute | solution.py:368
  76.0 10.4 %collective-permute-start.13 = (bf16[8,64,128]{2,1,0:T(8,128)(2,1)S(1)}, bf16[8,64,128]{2,1,0:T(8,128)(2,1)S(1)}, u32[]{:S(2)}, u32[]{:S(2)}) collective-permute-start(bf16[8,64,128]{2,1,0:T(8,128)(2,1)S(1)} %shard_map.62), channel_id=1, source_target_pairs={{0,64},{16,80},{32,96},{48,112},{64,0},{80,16},{96,32},{112,48},{1... | collective-permute-start | bytes 393224 | tf_op jit(solution)/shard_map/ppermute | solution.py:368
  79.8 8.4 %collective-permute-start.12 = (bf16[8,64,128]{2,1,0:T(8,128)(2,1)S(1)}, bf16[8,64,128]{2,1,0:T(8,128)(2,1)S(1)}, u32[]{:S(2)}, u32[]{:S(2)}) collective-permute-start(bf16[8,64,128]{2,1,0:T(8,128)(2,1)S(1)} %shard_map.62), channel_id=1, source_target_pairs={{0,48},{16,32},{32,16},{48,0},{64,112},{80,96},{96,80},{112,64},{1... | collective-permute-start | bytes 393224 | tf_op jit(solution)/shard_map/ppermute | solution.py:368
  83.7 5.4 %collective-permute-start.11 = (bf16[8,64,128]{2,1,0:T(8,128)(2,1)S(1)}, bf16[8,64,128]{2,1,0:T(8,128)(2,1)S(1)}, u32[]{:S(2)}, u32[]{:S(2)}) collective-permute-start(bf16[8,64,128]{2,1,0:T(8,128)(2,1)S(1)} %shard_map.62), channel_id=1, source_target_pairs={{0,32},{16,48},{32,0},{48,16},{64,96},{80,112},{96,64},{112,80},{1... | collective-permute-start | bytes 393224 | tf_op jit(solution)/shard_map/ppermute | solution.py:368
  83.9 5.2 %collective-permute-start.10 = (bf16[8,64,128]{2,1,0:T(8,128)(2,1)S(1)}, bf16[8,64,128]{2,1,0:T(8,128)(2,1)S(1)}, u32[]{:S(2)}, u32[]{:S(2)}) collective-permute-start(bf16[8,64,128]{2,1,0:T(8,128)(2,1)S(1)} %shard_map.62), channel_id=1, source_target_pairs={{0,16},{16,0},{32,48},{48,32},{64,80},{80,64},{96,112},{112,96},{1... | collective-permute-start | bytes 393224 | tf_op jit(solution)/shard_map/ppermute | solution.py:368
  91.9 6.3 %collective-permute-start.22 = (bf16[4,64,1024]{2,1,0:T(8,128)(2,1)S(1)}, bf16[4,64,1024]{2,1,0:T(8,128)(2,1)S(1)}, u32[]{:S(2)}, u32[]{:S(2)}) collective-permute-start(bf16[4,64,1024]{2,1,0:T(8,128)(2,1)S(1)} %shard_map.66), channel_id=1, source_target_pairs={{0,2},{2,0},{4,6},{6,4},{8,10},{10,8},{12,14},{14,12},{1,3},{3,1},... | collective-permute-start | bytes 1572872 | tf_op jit(solution)/shard_map/ppermute | solution.py:368
where the time goes:
time: 115 us; the launch traced here: 114 us
  starting transfers between devices  36.1 us (31%)
  Pallas kernels  30.1 us (26%)
  waiting for transfers between devices  27.1 us (24%)
  blocking collectives  14.7 us (13%)
  local copies, waits for them, and re-layouts  4.79 us (4%)
    ppermute x23, starting transfers between devices, send(): return lax.ppermute(x, axis, pairs)  32.6 us
    pallas_call x2, Pallas kernels, attention(): pl.pallas_call(functools.partial(attention_body, block=512, group=group,...  16.8 us
    ppermute x23, waiting for transfers between devices, send(): return lax.ppermute(x, axis, pairs)  16.6 us
    all_to_all x1, blocking collectives, spread(): return lax.all_to_all(x, 'tp', 0, 0, tiled=True, axis_index_groups=z_groups)  14.7 us
    pallas_call x12, Pallas kernels, small_call(): pl.pallas_call(body, grid_spec=pltpu.PrefetchScalarGridSpec(num_scalar_pr...  13.2 us
    all_to_all x1, waiting for transfers between devices, spread(): return lax.all_to_all(x, 'tp', 0, 0, tiled=True, axis_index_groups=z_groups)  10.4 us
    unnamed x14, local copies, waits for them, and re-layouts  4.79 us
    all_to_all x1, starting transfers between devices, spread(): return lax.all_to_all(x, 'tp', 0, 0, tiled=True, axis_index_groups=z_groups)  3.48 us
  transfers between devices with their start and end apart: 24, of which 12 were waited for; matrix products, arithmetic and copies ran while one was open for 0% of the time, Pallas kernels for 24%

commit v1 on v0

--- a/solution.py
+++ b/solution.py
@@ -78,7 +78,7 @@
         def scored(at):
             return lax.dot_general(
                 q,
-                kv_ref[0, at : at + block, :HD],
+                kv_ref[seq, at : at + block, :HD],
                 (((1,), (1,)), ((), ())),
                 preferred_element_type=jnp.float32,
             )
@@ -99,7 +99,7 @@
             weights = jnp.exp2((scores - new_top) * c2)
             if masked:
                 weights = jnp.where(visible, weights, 0.0)
-            values = kv_ref[0, at : at + block, HD:]
+            values = kv_ref[seq, at : at + block, HD:]
             both = jnp.concatenate([values, jnp.ones_like(values)], axis=1)
             sums = jnp.dot(weights.astype(jnp.bfloat16), both, preferred_element_type=jnp.float32)
             part, part_total = sums[:, :HD], sums[:, HD:]
@@ -141,17 +141,16 @@
     extent = kv.shape[1]
     shape = (group // 2, count + 1, tokens, HD)
     whole = pl.BlockSpec(memory_space=pltpu.VMEM)
-    block_of = lambda i, m: (place(lax.axis_index("tp") % 2, i), 0, 0)
     return pl.pallas_call(
         functools.partial(attention_body, block=512, group=group, place=place),
         grid_spec=pltpu.PrefetchScalarGridSpec(
             num_scalar_prefetch=1,
             grid=(count,),
-            in_specs=[whole] * len(parts) + [pl.BlockSpec((1, extent, 2 * HD), block_of)],
+            in_specs=[whole] * (len(parts) + 1),
             out_specs=[whole, whole],
         ),
         out_shape=[jax.ShapeDtypeStruct(shape, jnp.bfloat16)] * 2,
-        compiler_params=pltpu.CompilerParams(vmem_limit_bytes=50 * 1024 * 1024),
+        compiler_params=pltpu.CompilerParams(vmem_limit_bytes=36 * 1024 * 1024),
         cost_estimate=pl.CostEstimate(
             flops=count * tokens * group * extent * HD * 4,
             bytes_accessed=count * extent * 2 * HD * 2,
@@ -173,6 +172,34 @@
     return small_call(pack_rows_body, [own, other], [shape] * (own.shape[0] - 1), 5_000_000)
 
 
+def cut_query_body(q_ref, *cuts, chunks):
+    core = lax.axis_index("tp") % 2
+    count = cuts[0].shape[0]
+    for n, half in enumerate((core, 1 - core)):
+        for k in range(chunks):
+            cuts[n * chunks + k][...] = q_ref[pl.ds((half * chunks + k) * count, count)]
+
+
+def cut_query(query, chunks):
+    cut = jax.ShapeDtypeStruct((query.shape[0] // (2 * chunks),) + query.shape[1:], query.dtype)
+    body = functools.partial(cut_query_body, chunks=chunks)
+    return small_call(body, [query], [cut] * (2 * chunks), 1_000_000)
+
+
+def flag_body(head_of_slot, flag_ref, *, tests):
+    rank = lax.axis_index("tp")
+    head = head_of_slot[lax.axis_index("seq")]
+    for n, test in enumerate(tests):
+        outcome = jnp.where(test(rank % 2, rank // 2, head), 1, 0)
+        flag_ref[n] = jnp.full(flag_ref.shape[1:], outcome, jnp.int32)
+
+
+def flag(head_of_slot, tests):
+    flags = jax.ShapeDtypeStruct((len(tests), 8, 128), jnp.int32)
+    body = functools.partial(flag_body, tests=tests)
+    return small_call(body, [], [flags], 1_000, prefetch=(head_of_slot,))[0]
+
+
 def split_rows_body(w_ref, own_ref, other_ref):
     core = lax.axis_index("tp") % 2
     for v in range(w_ref.shape[0]):
@@ -181,44 +208,12 @@
 
 
 def split_rows(w):
-    shape = jax.ShapeDtypeStruct((w.shape[0],) + w.shape[2:], w.dtype)
-    return small_call(split_rows_body, [w], [shape, shape], 5_000_000)
-
-
-def cut_query_body(q_ref, *refs, chunks):
-    *outs, sems = refs
-    core = lax.axis_index("tp") % 2
-    count = outs[0].shape[0]
-    half = count * chunks
-    copies = []
-    for n, half_of in enumerate((core, 1 - core)):
-        for k in range(chunks):
-            source = q_ref.at[pl.ds(half_of * half + k * count, count)]
-            copies.append(pltpu.make_async_copy(source, outs[n * chunks + k], sems.at[n, k]))
-    for copy in copies:
-        copy.start()
-    for copy in copies:
-        copy.wait()
-
-
-def cut_query(query, chunks):
-    shape = jax.ShapeDtypeStruct((query.shape[0] // (2 * chunks),) + query.shape[1:], query.dtype)
-    return pl.pallas_call(
-        functools.partial(cut_query_body, chunks=chunks),
-        in_specs=[pl.BlockSpec(memory_space=pltpu.HBM)],
-        out_specs=[pl.BlockSpec(memory_space=pltpu.VMEM)] * (2 * chunks),
-        out_shape=[shape] * (2 * chunks),
-        scratch_shapes=[pltpu.SemaphoreType.DMA((2, chunks))],
-        compiler_params=pltpu.CompilerParams(vmem_limit_bytes=24 * 1024 * 1024),
-        cost_estimate=pl.CostEstimate(flops=1_000_000, bytes_accessed=4 * query.size, transcendentals=0),
-        name="cut_query",
-    )(query)
-
-
-def choose_body(head_of_slot, a_ref, b_ref, out_ref, *, first):
-    rank = lax.axis_index("tp")
-    head = head_of_slot[lax.axis_index("seq")]
-    take_first = first(rank % 2, rank // 2, head)
+    rows = jax.ShapeDtypeStruct((w.shape[0],) + w.shape[2:], w.dtype)
+    return small_call(split_rows_body, [w], [rows, rows], 5_000_000)
+
+
+def choose_body(flag_ref, a_ref, b_ref, out_ref, *, which):
+    take_first = jnp.max(flag_ref[which]) > 0
 
     @pl.when(take_first)
     def _():
@@ -229,10 +224,10 @@
         out_ref[...] = b_ref[...]
 
 
-def choose(head_of_slot, a, b, first):
+def choose(flags, a, b, which):
     shape = jax.ShapeDtypeStruct(a.shape, a.dtype)
-    body = functools.partial(choose_body, first=first)
-    return small_call(body, [a, b], [shape], 1_000_000, prefetch=(head_of_slot,))[0]
+    body = functools.partial(choose_body, which=which)
+    return small_call(body, [flags, a, b], [shape], 1_000_000)[0]
 
 
 def merge_shares(parts):
@@ -310,15 +305,11 @@
     )[0]
 
 
-def project_body(head_of_slot, *refs, count, own_parity):
-    pieces = refs[:count]
-    own_ref, came_ref, flip_ref, far_ref, far_hop_ref, mirror_ref, out_ref, w_ref = refs[count:]
-    tokens = pieces[0].shape[2]
-    half = pieces[0].shape[0]
+def assemble_body(head_of_slot, own_ref, came_ref, flip_ref, far_ref, far_hop_ref, mirror_ref, out_ref, w_ref):
+    half = own_ref.shape[0]
     seq_rank = lax.axis_index("seq")
     rank = lax.axis_index("tp")
     core, z = rank % 2, rank // 2
-    parity = core if own_parity else 1 - core
     w_ref[0, 0] = own_ref[z]
     w_ref[0, 1] = came_ref[z]
     w_ref[1] = flip_ref[...]
@@ -332,26 +323,40 @@
     def _():
         w_ref[2] = far_hop_ref[...]
 
-    x = jnp.concatenate([ref[:, parity].reshape(half * tokens, HD) for ref in pieces], axis=1)
-    rows = []
-    for k in range(count):
+    for k in range(2 * half):
         head = head_of_slot[seq_rank ^ k]
-        rows.append(w_ref[(head // 2) ^ z, (head % 2) ^ core])
-    y = jnp.dot(x, jnp.concatenate(rows, axis=0), preferred_element_type=jnp.float32)
-    out_ref[...] = y.reshape(out_ref.shape).astype(out_ref.dtype)
-
-
-def project(head_of_slot, pieces, blocks, own_parity, dtype):
-    count = len(pieces)
-    half, _, tokens, _ = pieces[0].shape
-    width = blocks[0].shape[-1]
+        out_ref[HD * k : HD * (k + 1)] = w_ref[(head // 2) ^ z, (head % 2) ^ core]
+
+
+def assemble(head_of_slot, blocks):
+    half, _, width = blocks[0].shape
     return small_call(
-        functools.partial(project_body, count=count, own_parity=own_parity),
-        [*pieces, *blocks],
-        [jax.ShapeDtypeStruct((half, tokens, width), dtype)],
-        2 * half * tokens * count * HD * width,
+        assemble_body,
+        blocks,
+        [jax.ShapeDtypeStruct((2 * half * HD, width), jnp.bfloat16)],
+        5_000_000,
         prefetch=(head_of_slot,),
         scratch=[pltpu.VMEM((half, 2, HD, width), jnp.bfloat16)],
+    )[0]
+
+
+def project_body(*refs, own_parity):
+    *pieces, w_ref, out_ref = refs
+    half, _, tokens, _ = pieces[0].shape
+    core = lax.axis_index("tp") % 2
+    parity = core if own_parity else 1 - core
+    x = jnp.concatenate([ref[:, parity].reshape(half * tokens, HD) for ref in pieces], axis=1)
+    y = jnp.dot(x, w_ref[...], preferred_element_type=jnp.float32)
+    out_ref[...] = y.reshape(out_ref.shape).astype(out_ref.dtype)
+
+
+def project(pieces, w, own_parity, dtype):
+    half, _, tokens, _ = pieces[0].shape
+    return small_call(
+        functools.partial(project_body, own_parity=own_parity),
+        [*pieces, w],
+        [jax.ShapeDtypeStruct((half, tokens, w.shape[1]), dtype)],
+        2 * half * tokens * w.size,
     )[0]
 
 
@@ -388,12 +393,13 @@
 
     chunk = half // CHUNKS
     cuts = cut_query(query, CHUNKS)
+    flags = flag(head_of_slot, (owned, unreached, reached))
     came = [send(cuts[n], "tp", swap_core) for n in range(CHUNKS)]
-    parts = [choose(head_of_slot, cuts[CHUNKS + n], new, owned) for n, new in enumerate(came)]
+    parts = [choose(flags, cuts[CHUNKS + n], new, 0) for n, new in enumerate(came)]
     came = [send(part, "tp", first_hop) for part in parts]
-    parts = [choose(head_of_slot, part, new, unreached) for new, part in zip(came, parts)]
+    parts = [choose(flags, part, new, 1) for new, part in zip(came, parts)]
     came = [send(part, "tp", second_hop) for part in parts]
-    parts = [choose(head_of_slot, part, new, reached) for new, part in zip(came, parts)]
+    parts = [choose(flags, part, new, 2) for new, part in zip(came, parts)]
     rest = [send(part, "tp", swap_core) for part in parts]
     own, other = split_rows(out_weight.reshape(chips, 2, HD, out_weight.shape[1]))
     swapped = send(other, "tp", swap_core)
@@ -409,19 +415,23 @@
 
     def later(core, step):
         own_half = (1 - core) * half + chunk + step
-        return jnp.where(step < left, own_half, core * half + step - left)
+        return jnp.where(step < left, own_half, core * half + chunk + step - left)
 
     first = attention(lengths, parts[:1], kv, group, lambda core, step: (1 - core) * half + step)
     first_came = send(first[0], "tp", swap_core)
-    second = attention(lengths, parts[1:] + rest, kv, group, later)
+    second = attention(lengths, rest[:1], kv, group, lambda core, step: core * half + step)
     second_came = send(second[0], "tp", swap_core)
+    third = attention(lengths, parts[1:] + rest[1:], kv, group, later)
+    third_came = send(third[0], "tp", swap_core)
     groups = (
-        (2, left, 1, 0, True, 0, chunk),
-        (2, half, 3, 0, True, chunk, left),
-        (0, 0, 3, left, False, 0, chunk),
-        (2, 0, 3, half, False, chunk, left),
+        (2, 0, 1, 0, True, 0, chunk),
+        (4, left, 5, 0, True, chunk, left),
+        (0, 0, 3, 0, False, 0, chunk),
+        (4, 0, 5, left, False, chunk, left),
     )
-    by_chip = merge_pair([first[1], first_came, second[1], second_came], groups, seqs)
+    by_chip = merge_pair(
+        [first[1], first_came, second[1], second_came, third[1], third_came], groups, seqs
+    )
     z_groups = [[2 * v + c for v in ring] for c in range(2)]
 
     def spread(x):
@@ -431,9 +441,10 @@
 
     pieces = [piece] + [send(piece, "seq", [(i, i ^ k) for i in range(seq_size)]) for k in range(1, seq_size)]
     pieces = [p.reshape(chips, 2, tokens, HD) for p in pieces]
-    sent = project(head_of_slot, pieces, blocks, False, jnp.bfloat16)
+    w = assemble(head_of_slot, blocks)
+    sent = project(pieces, w, False, jnp.bfloat16)
     came = send(sent, "tp", swap_core)
-    kept = project(head_of_slot, pieces, blocks, True, jnp.float32)
+    kept = project(pieces, w, True, jnp.float32)
     sums = (kept + came.astype(jnp.float32)).astype(jnp.bfloat16)
     arrived = spread(sums)
     return jnp.sum(arrived.astype(jnp.float32), axis=0, keepdims=True).astype(jnp.bfloat16)

time: 115 us -> 104 us (0.904)
  Pallas kernels: 30.1 us -> 24.5 us
  waiting for transfers between devices: 27.1 us -> 23.3 us
  blocking collectives: 14.7 us -> 12.1 us
  starting transfers between devices: 36.1 us -> 37.4 us
    all_to_all x1, waiting for transfers between devices: 10.4 us -> 4.14 us  [spread(): return lax.all_to_all(x, 'tp', 0, 0, tiled=True, axis_index_groups=z_groups)]
    pallas_call x12 -> x15, Pallas kernels: 13.2 us -> 9.62 us  [small_call(): pl.pallas_call(body, grid_spec=pltpu.PrefetchScalarGridSpec(num_scalar_pr...]
    ppermute x23 -> x24, waiting for transfers between devices: 16.6 us -> 19.2 us  [send(): return lax.ppermute(x, axis, pairs)]
    all_to_all x1, blocking collectives: 14.7 us -> 12.1 us  [spread(): return lax.all_to_all(x, 'tp', 0, 0, tiled=True, axis_index_groups=z_groups)]
    pallas_call x2 -> x3, Pallas kernels: 16.8 us -> 14.9 us  [attention(): pl.pallas_call(functools.partial(attention_body, block=512, group=group,...]
    ppermute x23 -> x24, starting transfers between devices: 32.6 us -> 33.9 us  [send(): return lax.ppermute(x, axis, pairs)]
  transfers between devices with their start and end apart: 24 -> 25, of which waited for: 12 -> 11; matrix products, arithmetic and copies ran while one was open for 0% -> 0% of each run, Pallas kernels for 24% -> 23%
where the time goes in v1:
time: 104 us
  starting transfers between devices  37.4 us (36%)
  Pallas kernels  24.5 us (24%)
  waiting for transfers between devices  23.3 us (22%)
  blocking collectives  12.1 us (12%)
  local copies, waits for them, and re-layouts  5.1 us (5%)
    ppermute x24, starting transfers between devices, send(): return lax.ppermute(x, axis, pairs)  33.9 us
    ppermute x24, waiting for transfers between devices, send(): return lax.ppermute(x, axis, pairs)  19.2 us
    pallas_call x3, Pallas kernels, attention(): pl.pallas_call(functools.partial(attention_body, block=512, group=group,...  14.9 us
    all_to_all x1, blocking collectives, spread(): return lax.all_to_all(x, 'tp', 0, 0, tiled=True, axis_index_groups=z_groups)  12.1 us
    pallas_call x15, Pallas kernels, small_call(): pl.pallas_call(body, grid_spec=pltpu.PrefetchScalarGridSpec(num_scalar_pr...  9.62 us
    unnamed x14, local copies, waits for them, and re-layouts  5.1 us
    all_to_all x1, waiting for transfers between devices, spread(): return lax.all_to_all(x, 'tp', 0, 0, tiled=True, axis_index_groups=z_groups)  4.14 us
    all_to_all x1, starting transfers between devices, spread(): return lax.all_to_all(x, 'tp', 0, 0, tiled=True, axis_index_groups=z_groups)  3.48 us
  transfers between devices with their start and end apart: 25, of which 11 were waited for; matrix products, arithmetic and copies ran while one was open for 0% of the time, Pallas kernels for 23%

profile of v1, /device:TPU:1, one launch (start us, length us, event | category | flops | bytes accessed | tf_op | source)
XLA Modules:
  0.0 103.6 jit_solution(6537008845434062240)
XLA Ops:
  0.0 1.6 %copy-done.1 = bf16[1024,1024]{1,0:T(8,128)(2,1)S(1)} copy-done((bf16[1024,1024]{1,0:T(8,128)(2,1)S(1)}, bf16[1024,1024]{1,0:T(8,128)(2,1)}, u32[]{:S(2)}) %copy-start.1) | copy-done | bytes 2097176
  1.7 1.5 %collective-permute-start.18 = (bf16[4,128,1024]{2,1,0:T(8,128)(2,1)S(1)}, bf16[4,128,1024]{2,1,0:T(8,128)(2,1)S(1)}, u32[]{:S(2)}, u32[]{:S(2)}) collective-permute-start(bf16[4,128,1024]{2,1,0:T(8,128)(2,1)S(1)} %get-tuple-element.31), channel_id=1, source_target_pairs={{0,2},{2,0},{4,6},{6,4},{8,10},{10,8},{12,14},{14,12},{1,3},{3,1},... | collective-permute-start | bytes 3145736 | tf_op jit(solution)/shard_map/ppermute | solution.py:373
  3.2 1.9 %copy-done.2 = bf16[8,64,1024]{2,1,0:T(8,128)(2,1)S(1)} copy-done((bf16[8,64,1024]{2,1,0:T(8,128)(2,1)S(1)}, bf16[8,64,1024]{2,1,0:T(8,128)(2,1)}, u32[]{:S(2)}) %copy-start.2) | copy-done | bytes 1048600
  5.3 0.5 collective-permute-start
  5.8 0.6 shard_map.55.flag_ref
  6.3 0.4 collective-permute-done.6.b_ref
  7.0 3.7 %collective-permute-start.7 = (bf16[2,64,1024]{2,1,0:T(8,128)(2,1)S(1)}, bf16[2,64,1024]{2,1,0:T(8,128)(2,1)S(1)}, u32[]{:S(2)}, u32[]{:S(2)}) collective-permute-start(bf16[2,64,1024]{2,1,0:T(8,128)(2,1)S(1)} %shard_map.60.a_ref), channel_id=1, source_target_pairs={{0,4},{4,0},{8,12},{12,8},{2,14},{6,10},{10,6},{14,2},{1,5},{5,1},... | collective-permute-start | bytes 786440 | tf_op jit(solution)/shard_map/ppermute | solution.py:373
  10.7 0.2 shard_map.57.a_ref
  11.0 3.4 %collective-permute-done.7.b_ref = bf16[2,64,1024]{2,1,0:T(8,128)(2,1)S(1)} collective-permute-done((bf16[2,64,1024]{2,1,0:T(8,128)(2,1)S(1)}, bf16[2,64,1024]{2,1,0:T(8,128)(2,1)S(1)}, u32[]{:S(2)}, u32[]{:S(2)}) %collective-permute-start.7) | collective-permute-done | bytes 262176 | tf_op jit(solution)/shard_map/ppermute | solution.py:373
  14.4 0.2 shard_map.61.a_ref
  14.8 2.6 %collective-permute-done.1.b_ref = bf16[2,64,1024]{2,1,0:T(8,128)(2,1)S(1)} collective-permute-done((bf16[2,64,1024]{2,1,0:T(8,128)(2,1)S(1)}, bf16[2,64,1024]{2,1,0:T(8,128)(2,1)S(1)}, u32[]{:S(2)}, u32[]{:S(2)}) %collective-permute-start.1) | collective-permute-done | bytes 262176 | tf_op jit(solution)/shard_map/ppermute | solution.py:373
  17.7 2.5 %collective-permute-done.8.b_ref = bf16[2,64,1024]{2,1,0:T(8,128)(2,1)S(1)} collective-permute-done((bf16[2,64,1024]{2,1,0:T(8,128)(2,1)S(1)}, bf16[2,64,1024]{2,1,0:T(8,128)(2,1)S(1)}, u32[]{:S(2)}, u32[]{:S(2)}) %collective-permute-start.8) | collective-permute-done | bytes 262176 | tf_op jit(solution)/shard_map/ppermute | solution.py:373
  20.5 1.9 %collective-permute-start.9 = (bf16[2,64,1024]{2,1,0:T(8,128)(2,1)S(1)}, bf16[2,64,1024]{2,1,0:T(8,128)(2,1)S(1)}, u32[]{:S(2)}, u32[]{:S(2)}) collective-permute-start(bf16[2,64,1024]{2,1,0:T(8,128)(2,1)S(1)} %shard_map.62.refs_0_), channel_id=1, source_target_pairs={{0,2},{2,0},{4,6},{6,4},{8,10},{10,8},{12,14},{14,12},{1,3},{3,1},... | collective-permute-start | bytes 786440 | tf_op jit(solution)/shard_map/ppermute | solution.py:373
  22.4 0.8 collective-permute-done.2.b_ref
  23.5 2.5 %collective-permute-start.4 = (bf16[2,64,1024]{2,1,0:T(8,128)(2,1)S(1)}, bf16[2,64,1024]{2,1,0:T(8,128)(2,1)S(1)}, u32[]{:S(2)}, u32[]{:S(2)}) collective-permute-start(bf16[2,64,1024]{2,1,0:T(8,128)(2,1)S(1)} %shard_map.59.refs_0_), channel_id=1, source_target_pairs={{0,2},{2,0},{4,6},{6,4},{8,10},{10,8},{12,14},{14,12},{1,3},{3,1},... | collective-permute-start | bytes 786440 | tf_op jit(solution)/shard_map/ppermute | solution.py:373
  26.0 0.9 shard_map.66
  26.9 0.8 copy-done.5
  27.7 0.8 copy-done.6
  28.5 2.2 %collective-permute-start.20 = (bf16[2,128,1024]{2,1,0:T(8,128)(2,1)}, bf16[2,128,1024]{2,1,0:T(8,128)(2,1)S(1)}, u32[]{:S(2)}, u32[]{:S(2)}) collective-permute-start(bf16[2,128,1024]{2,1,0:T(8,128)(2,1)} %get-tuple-element.33), channel_id=1, source_target_pairs={{0,8},{4,12},{8,0},{12,4},{2,14},{6,2},{10,6},{14,10},{1,9},{5,13}... | collective-permute-start | bytes 1572872 | tf_op jit(solution)/shard_map/ppermute | solution.py:373
  30.7 7.2 %attend.5 = (bf16[4,5,64,128]{3,2,1,0:T(8,128)(2,1)S(1)}, bf16[4,5,64,128]{3,2,1,0:T(8,128)(2,1)S(1)}) custom-call(s32[8]{0:T(128)S(1)} %copy-done.3, bf16[2,64,1024]{2,1,0:T(8,128)(2,1)S(1)} %shard_map.62.refs_0_, bf16[2,64,1024]{2,1,0:T(8,128)(2,1)S(1)} %collective-permute-done.9.refs_1_, bf16[8,2048,256]{2,1,0:T(8,128)(2,1)S(1)} %bitcast.11), custom_call_target="tpu_custom_call" | custom-call | flops 2147483648 | bytes 4194304 | tf_op jit(solution)/shard_map/attend/pallas_call | solution.py:144
  38.0 3.9 %attend.3 = (bf16[4,3,64,128]{3,2,1,0:T(8,128)(2,1)S(1)}, bf16[4,3,64,128]{3,2,1,0:T(8,128)(2,1)S(1)}) custom-call(s32[8]{0:T(128)S(1)} %copy-done.3, bf16[2,64,1024]{2,1,0:T(8,128)(2,1)S(1)} %shard_map.59.refs_0_, bf16[8,2048,256]{2,1,0:T(8,128)(2,1)S(1)} %bitcast.12), custom_call_target="tpu_custom_call" | custom-call | flops 1073741824 | bytes 2097152 | tf_op jit(solution)/shard_map/attend/pallas_call | solution.py:144
  41.8 0.8 collective-permute-start.3
  42.6 3.9 %attend.4 = (bf16[4,3,64,128]{3,2,1,0:T(8,128)(2,1)S(1)}, bf16[4,3,64,128]{3,2,1,0:T(8,128)(2,1)S(1)}) custom-call(s32[8]{0:T(128)S(1)} %copy-done.3, bf16[2,64,1024]{2,1,0:T(8,128)(2,1)S(1)} %collective-permute-done.4.refs_0_, bf16[8,2048,256]{2,1,0:T(8,128)(2,1)S(1)} %bitcast.13), custom_call_target="tpu_custom_call" | custom-call | flops 1073741824 | bytes 2097152 | tf_op jit(solution)/shard_map/attend/pallas_call | solution.py:144
  46.6 1.4 %collective-permute-done.5.refs_3_ = bf16[4,3,64,128]{3,2,1,0:T(8,128)(2,1)S(1)} collective-permute-done((bf16[4,3,64,128]{3,2,1,0:T(8,128)(2,1)S(1)}, bf16[4,3,64,128]{3,2,1,0:T(8,128)(2,1)S(1)}, u32[]{:S(2)}, u32[]{:S(2)}) %collective-permute-start.5) | collective-permute-done | bytes 196640 | tf_op jit(solution)/shard_map/ppermute | solution.py:373
  48.0 2.6 %shard_map.63 = bf16[4,9,64,128]{3,2,1,0:T(8,128)(2,1)} custom-call(bf16[4,3,64,128]{3,2,1,0:T(8,128)(2,1)S(1)} %get-tuple-element.22.refs_0_, bf16[4,3,64,128]{3,2,1,0:T(8,128)(2,1)S(1)} %collective-permute-done.3.refs_1_, bf16[4,3,64,128]{3,2,1,0:T(8,128)(2,1)S(1)} %get-tuple-element.24.refs_2_, ...), custom_call_target="tpu_custom_call" | custom-call | flops 40000000 | bytes 2000000 | tf_op jit(solution)/shard_map/pallas_call | solution.py:243
  50.5 3.5 %all-to-all-start = ((bf16[4,9,64,128]{3,2,1,0:T(8,128)(2,1)}), bf16[4,9,64,128]{3,2,1,0:T(8,128)(2,1)S(1)}, u32[]{:S(2)}, u32[]{:S(2)}) async-start(bf16[4,9,64,128]{3,2,1,0:T(8,128)(2,1)} %shard_map.63), calls=%async_computation | async-start | bytes 1179648 | tf_op jit(solution)/shard_map/all_to_all | solution.py:438
  54.0 1.4 %collective-permute-start.19 = (bf16[2,128,1024]{2,1,0:T(8,128)(2,1)}, bf16[2,128,1024]{2,1,0:T(8,128)(2,1)}, u32[]{:S(2)}, u32[]{:S(2)}) collective-permute-start(bf16[2,128,1024]{2,1,0:T(8,128)(2,1)} %copy-done.6), channel_id=1, source_target_pairs={{0,4},{2,6},{4,0},{6,2},{8,12},{10,14},{12,8},{14,10},{1,5},{3,7},... | collective-permute-start | bytes 1572872 | tf_op jit(solution)/shard_map/ppermute | solution.py:373
  55.5 1.8 %collective-permute-start.22 = (bf16[2,128,1024]{2,1,0:T(8,128)(2,1)}, bf16[2,128,1024]{2,1,0:T(8,128)(2,1)}, u32[]{:S(2)}, u32[]{:S(2)}) collective-permute-start(bf16[2,128,1024]{2,1,0:T(8,128)(2,1)} %copy-done.5), channel_id=1, source_target_pairs={{0,12},{2,14},{4,8},{6,10},{8,4},{10,6},{12,0},{14,2},{1,13},{3,15... | collective-permute-start | bytes 1572872 | tf_op jit(solution)/shard_map/ppermute | solution.py:373
  57.2 2.8 %collective-permute-start.21 = (bf16[2,128,1024]{2,1,0:T(8,128)(2,1)S(1)}, bf16[2,128,1024]{2,1,0:T(8,128)(2,1)}, u32[]{:S(2)}, u32[]{:S(2)}) collective-permute-start(bf16[2,128,1024]{2,1,0:T(8,128)(2,1)S(1)} %collective-permute-done.20.far_ref), channel_id=1, source_target_pairs={{2,14},{6,2},{10,6},{14,10},{3,15},{7,3},{11,7},{15,11},{18,30},{2... | collective-permute-start | bytes 1572872 | tf_op jit(solution)/shard_map/ppermute | solution.py:373
  60.0 4.1 %all-to-all-done.x_ref = bf16[4,9,64,128]{3,2,1,0:T(8,128)(2,1)S(1)} async-done(((bf16[4,9,64,128]{3,2,1,0:T(8,128)(2,1)}), bf16[4,9,64,128]{3,2,1,0:T(8,128)(2,1)S(1)}, u32[]{:S(2)}, u32[]{:S(2)}) %all-to-all-start) | async-done | bytes 589856 | tf_op jit(solution)/shard_map/all_to_all | solution.py:438
  64.2 0.5 shard_map.64
  64.7 3.6 %collective-permute-start.17 = (bf16[8,64,128]{2,1,0:T(8,128)(2,1)S(1)}, bf16[8,64,128]{2,1,0:T(8,128)(2,1)S(1)}, u32[]{:S(2)}, u32[]{:S(2)}) collective-permute-start(bf16[8,64,128]{2,1,0:T(8,128)(2,1)S(1)} %shard_map.64), channel_id=1, source_target_pairs={{0,112},{16,96},{32,80},{48,64},{64,48},{80,32},{96,16},{112,0},{1... | collective-permute-start | bytes 393224 | tf_op jit(solution)/shard_map/ppermute | solution.py:373
  68.2 0.4 collective-permute-start.16
  68.7 5.4 %collective-permute-done.19.flip_ref = bf16[2,128,1024]{2,1,0:T(8,128)(2,1)} collective-permute-done((bf16[2,128,1024]{2,1,0:T(8,128)(2,1)}, bf16[2,128,1024]{2,1,0:T(8,128)(2,1)}, u32[]{:S(2)}, u32[]{:S(2)}) %collective-permute-start.19) | collective-permute-done | bytes 524320 | tf_op jit(solution)/shard_map/ppermute | solution.py:373
  74.0 2.2 %collective-permute-start.15 = (bf16[8,64,128]{2,1,0:T(8,128)(2,1)S(1)}, bf16[8,64,128]{2,1,0:T(8,128)(2,1)S(1)}, u32[]{:S(2)}, u32[]{:S(2)}) collective-permute-start(bf16[8,64,128]{2,1,0:T(8,128)(2,1)S(1)} %shard_map.64), channel_id=1, source_target_pairs={{0,80},{16,64},{32,112},{48,96},{64,16},{80,0},{96,48},{112,32},{1... | collective-permute-start | bytes 393224 | tf_op jit(solution)/shard_map/ppermute | solution.py:373
  76.2 0.2 collective-permute-start.14
  76.5 2.5 %collective-permute-start.13 = (bf16[8,64,128]{2,1,0:T(8,128)(2,1)S(1)}, bf16[8,64,128]{2,1,0:T(8,128)(2,1)S(1)}, u32[]{:S(2)}, u32[]{:S(2)}) collective-permute-start(bf16[8,64,128]{2,1,0:T(8,128)(2,1)S(1)} %shard_map.64), channel_id=1, source_target_pairs={{0,48},{16,32},{32,16},{48,0},{64,112},{80,96},{96,80},{112,64},{1... | collective-permute-start | bytes 393224 | tf_op jit(solution)/shard_map/ppermute | solution.py:373
  79.0 0.5 collective-permute-start.12
  79.5 0.6 collective-permute-done.21.far_hop_ref
  80.1 1.2 %collective-permute-start.11 = (bf16[8,64,128]{2,1,0:T(8,128)(2,1)S(1)}, bf16[8,64,128]{2,1,0:T(8,128)(2,1)S(1)}, u32[]{:S(2)}, u32[]{:S(2)}) collective-permute-start(bf16[8,64,128]{2,1,0:T(8,128)(2,1)S(1)} %shard_map.64), channel_id=1, source_target_pairs={{0,16},{16,0},{32,48},{48,32},{64,80},{80,64},{96,112},{112,96},{1... | collective-permute-start | bytes 393224 | tf_op jit(solution)/shard_map/ppermute | solution.py:373
  81.3 2.2 %shard_map.67.refs_8_ = bf16[1024,1024]{1,0:T(8,128)(2,1)S(1)} custom-call(s32[8]{0:T(128)S(1)} %copy-done.4, bf16[4,128,1024]{2,1,0:T(8,128)(2,1)S(1)} %get-tuple-element.30.own_ref, bf16[4,128,1024]{2,1,0:T(8,128)(2,1)S(1)} %collective-permute-done.18.other_ref.came_ref, bf16[2,128,1024]{2,1,0:T(8,128)(2,1)} %collective-permute-done.19.flip_ref, ...), custom_call_target="tpu_custom_call" | custom-call | flops 5000000 | bytes 2000000 | tf_op jit(solution)/shard_map/pallas_call | solution.py:243
  83.6 1.1 %collective-permute-done.12 = bf16[8,64,128]{2,1,0:T(8,128)(2,1)S(1)} collective-permute-done((bf16[8,64,128]{2,1,0:T(8,128)(2,1)S(1)}, bf16[8,64,128]{2,1,0:T(8,128)(2,1)S(1)}, u32[]{:S(2)}, u32[]{:S(2)}) %collective-permute-start.12) | collective-permute-done | bytes 131104 | tf_op jit(solution)/shard_map/ppermute | solution.py:373
  84.7 0.7 shard_map.69
  85.4 3.6 %collective-permute-start.23 = (bf16[4,64,1024]{2,1,0:T(8,128)(2,1)S(1)}, bf16[4,64,1024]{2,1,0:T(8,128)(2,1)S(1)}, u32[]{:S(2)}, u32[]{:S(2)}) collective-permute-start(bf16[4,64,1024]{2,1,0:T(8,128)(2,1)S(1)} %shard_map.69), channel_id=1, source_target_pairs={{0,2},{2,0},{4,6},{6,4},{8,10},{10,8},{12,14},{14,12},{1,3},{3,1},... | collective-permute-start | bytes 1572872 | tf_op jit(solution)/shard_map/ppermute | solution.py:373
  89.0 0.7 shard_map.68
  89.7 0.8 collective-permute-done.23
  90.7 12.1 %all_to_all.10 = bf16[4,64,1024]{2,1,0:T(8,128)(2,1)S(1)} all-to-all(bf16[4,64,1024]{2,1,0:T(8,128)(2,1)S(1)} %add_convert_fusion), channel_id=1, replica_groups={{0,4,8,12},{2,6,10,14},{1,5,9,13},{3,7,11,15},{16,20,24,28},{18,22,26,3..., dimensions={0} | all-to-all | bytes 1048576 | tf_op jit(solution)/shard_map/all_to_all | solution.py:438
  102.8 0.7 reduce_sum.12
  (37 shorter events, 1.9 us)
Async XLA Ops:
  0.0 5.8 %copy-start.4 = (s32[8]{0:T(128)S(1)}, s32[8]{0:T(128)}, u32[]{:S(2)}) copy-start(s32[8]{0:T(128)} %head_of_slot.3) | copy-start | bytes 100
  0.0 1.6 %copy-start.1 = (bf16[1024,1024]{1,0:T(8,128)(2,1)S(1)}, bf16[1024,1024]{1,0:T(8,128)(2,1)}, u32[]{:S(2)}) copy-start(bf16[1024,1024]{1,0:T(8,128)(2,1)} %param.9) | copy-start | bytes 6291460
  1.6 29.1 %copy-start = (bf16[8,2048,1,256]{3,1,2,0:T(8,128)(2,1)S(1)}, bf16[8,2048,1,256]{3,1,2,0:T(8,128)(2,1)}, u32[]{:S(2)}) copy-start(bf16[8,2048,1,256]{3,1,2,0:T(8,128)(2,1)} %param.6) | copy-start | bytes 25165828
  1.7 24.2 %collective-permute-start.18 = (bf16[4,128,1024]{2,1,0:T(8,128)(2,1)S(1)}, bf16[4,128,1024]{2,1,0:T(8,128)(2,1)S(1)}, u32[]{:S(2)}, u32[]{:S(2)}) collective-permute-start(bf16[4,128,1024]{2,1,0:T(8,128)(2,1)S(1)} %get-tuple-element.31), channel_id=1, source_target_pairs={{0,2},{2,0},{4,6},{6,4},{8,10},{10,8},{12,14},{14,12},{1,3},{3,1},... | collective-permute-start | bytes 3145736 | tf_op jit(solution)/shard_map/ppermute | solution.py:373
  3.2 1.9 %copy-start.2 = (bf16[8,64,1024]{2,1,0:T(8,128)(2,1)S(1)}, bf16[8,64,1024]{2,1,0:T(8,128)(2,1)}, u32[]{:S(2)}) copy-start(bf16[8,64,1024]{2,1,0:T(8,128)(2,1)} %q_ref.1) | copy-start | bytes 3145732
  5.2 1.6 %collective-permute-start.6 = (bf16[2,64,1024]{2,1,0:T(8,128)(2,1)S(1)}, bf16[2,64,1024]{2,1,0:T(8,128)(2,1)S(1)}, u32[]{:S(2)}, u32[]{:S(2)}) collective-permute-start(bf16[2,64,1024]{2,1,0:T(8,128)(2,1)S(1)} %get-tuple-element.27), channel_id=1, source_target_pairs={{0,2},{2,0},{4,6},{6,4},{8,10},{10,8},{12,14},{14,12},{1,3},{3,1},... | collective-permute-start | bytes 786440 | tf_op jit(solution)/shard_map/ppermute | solution.py:373
  5.3 5.4 %collective-permute-start = (bf16[2,64,1024]{2,1,0:T(8,128)(2,1)S(1)}, bf16[2,64,1024]{2,1,0:T(8,128)(2,1)S(1)}, u32[]{:S(2)}, u32[]{:S(2)}) collective-permute-start(bf16[2,64,1024]{2,1,0:T(8,128)(2,1)S(1)} %get-tuple-element.21), channel_id=1, source_target_pairs={{0,2},{2,0},{4,6},{6,4},{8,10},{10,8},{12,14},{14,12},{1,3},{3,1},... | collective-permute-start | bytes 786440 | tf_op jit(solution)/shard_map/ppermute | solution.py:373
  7.0 7.4 %collective-permute-start.7 = (bf16[2,64,1024]{2,1,0:T(8,128)(2,1)S(1)}, bf16[2,64,1024]{2,1,0:T(8,128)(2,1)S(1)}, u32[]{:S(2)}, u32[]{:S(2)}) collective-permute-start(bf16[2,64,1024]{2,1,0:T(8,128)(2,1)S(1)} %shard_map.60.a_ref), channel_id=1, source_target_pairs={{0,4},{4,0},{8,12},{12,8},{2,14},{6,10},{10,6},{14,2},{1,5},{5,1},... | collective-permute-start | bytes 786440 | tf_op jit(solution)/shard_map/ppermute | solution.py:373
  10.9 6.5 %collective-permute-start.1 = (bf16[2,64,1024]{2,1,0:T(8,128)(2,1)S(1)}, bf16[2,64,1024]{2,1,0:T(8,128)(2,1)S(1)}, u32[]{:S(2)}, u32[]{:S(2)}) collective-permute-start(bf16[2,64,1024]{2,1,0:T(8,128)(2,1)S(1)} %shard_map.57.a_ref), channel_id=1, source_target_pairs={{0,4},{4,0},{8,12},{12,8},{2,14},{6,10},{10,6},{14,2},{1,5},{5,1},... | collective-permute-start | bytes 786440 | tf_op jit(solution)/shard_map/ppermute | solution.py:373
  14.7 16.1 %copy-start.3 = (s32[8]{0:T(128)S(1)}, s32[8]{0:T(128)}, u32[]{:S(2)}) copy-start(s32[8]{0:T(128)} %lengths.5) | copy-start | bytes 100
  14.7 5.6 %collective-permute-start.8 = (bf16[2,64,1024]{2,1,0:T(8,128)(2,1)S(1)}, bf16[2,64,1024]{2,1,0:T(8,128)(2,1)S(1)}, u32[]{:S(2)}, u32[]{:S(2)}) collective-permute-start(bf16[2,64,1024]{2,1,0:T(8,128)(2,1)S(1)} %shard_map.61.a_ref), channel_id=1, source_target_pairs={{0,12},{4,8},{8,4},{12,0},{2,6},{6,2},{10,14},{14,10},{1,13},{5,9}... | collective-permute-start | bytes 786440 | tf_op jit(solution)/shard_map/ppermute | solution.py:373
  17.6 5.6 %collective-permute-start.2 = (bf16[2,64,1024]{2,1,0:T(8,128)(2,1)S(1)}, bf16[2,64,1024]{2,1,0:T(8,128)(2,1)S(1)}, u32[]{:S(2)}, u32[]{:S(2)}) collective-permute-start(bf16[2,64,1024]{2,1,0:T(8,128)(2,1)S(1)} %shard_map.58.a_ref), channel_id=1, source_target_pairs={{0,12},{4,8},{8,4},{12,0},{2,6},{6,2},{10,14},{14,10},{1,13},{5,9}... | collective-permute-start | bytes 786440 | tf_op jit(solution)/shard_map/ppermute | solution.py:373
  20.5 10.2 %collective-permute-start.9 = (bf16[2,64,1024]{2,1,0:T(8,128)(2,1)S(1)}, bf16[2,64,1024]{2,1,0:T(8,128)(2,1)S(1)}, u32[]{:S(2)}, u32[]{:S(2)}) collective-permute-start(bf16[2,64,1024]{2,1,0:T(8,128)(2,1)S(1)} %shard_map.62.refs_0_), channel_id=1, source_target_pairs={{0,2},{2,0},{4,6},{6,4},{8,10},{10,8},{12,14},{14,12},{1,3},{3,1},... | collective-permute-start | bytes 786440 | tf_op jit(solution)/shard_map/ppermute | solution.py:373
  23.5 19.1 %collective-permute-start.4 = (bf16[2,64,1024]{2,1,0:T(8,128)(2,1)S(1)}, bf16[2,64,1024]{2,1,0:T(8,128)(2,1)S(1)}, u32[]{:S(2)}, u32[]{:S(2)}) collective-permute-start(bf16[2,64,1024]{2,1,0:T(8,128)(2,1)S(1)} %shard_map.59.refs_0_), channel_id=1, source_target_pairs={{0,2},{2,0},{4,6},{6,4},{8,10},{10,8},{12,14},{14,12},{1,3},{3,1},... | collective-permute-start | bytes 786440 | tf_op jit(solution)/shard_map/ppermute | solution.py:373
  26.9 0.8 copy-start.5
  27.7 0.8 copy-start.6
  28.5 28.8 %collective-permute-start.20 = (bf16[2,128,1024]{2,1,0:T(8,128)(2,1)}, bf16[2,128,1024]{2,1,0:T(8,128)(2,1)S(1)}, u32[]{:S(2)}, u32[]{:S(2)}) collective-permute-start(bf16[2,128,1024]{2,1,0:T(8,128)(2,1)} %get-tuple-element.33), channel_id=1, source_target_pairs={{0,8},{4,12},{8,0},{12,4},{2,14},{6,2},{10,6},{14,10},{1,9},{5,13}... | collective-permute-start | bytes 1572872 | tf_op jit(solution)/shard_map/ppermute | solution.py:373
  37.9 10.1 %collective-permute-start.10 = (bf16[4,5,64,128]{3,2,1,0:T(8,128)(2,1)S(1)}, bf16[4,5,64,128]{3,2,1,0:T(8,128)(2,1)S(1)}, u32[]{:S(2)}, u32[]{:S(2)}) collective-permute-start(bf16[4,5,64,128]{3,2,1,0:T(8,128)(2,1)S(1)} %get-tuple-element.29), channel_id=1, source_target_pairs={{0,2},{2,0},{4,6},{6,4},{8,10},{10,8},{12,14},{14,12},{1,3},{3,1},... | collective-permute-start | bytes 983048 | tf_op jit(solution)/shard_map/ppermute | solution.py:373
  41.8 4.7 %collective-permute-start.3 = (bf16[4,3,64,128]{3,2,1,0:T(8,128)(2,1)S(1)}, bf16[4,3,64,128]{3,2,1,0:T(8,128)(2,1)S(1)}, u32[]{:S(2)}, u32[]{:S(2)}) collective-permute-start(bf16[4,3,64,128]{3,2,1,0:T(8,128)(2,1)S(1)} %get-tuple-element.23), channel_id=1, source_target_pairs={{0,2},{2,0},{4,6},{6,4},{8,10},{10,8},{12,14},{14,12},{1,3},{3,1},... | collective-permute-start | bytes 589832 | tf_op jit(solution)/shard_map/ppermute | solution.py:373
  46.5 1.5 %collective-permute-start.5 = (bf16[4,3,64,128]{3,2,1,0:T(8,128)(2,1)S(1)}, bf16[4,3,64,128]{3,2,1,0:T(8,128)(2,1)S(1)}, u32[]{:S(2)}, u32[]{:S(2)}) collective-permute-start(bf16[4,3,64,128]{3,2,1,0:T(8,128)(2,1)S(1)} %get-tuple-element.25), channel_id=1, source_target_pairs={{0,2},{2,0},{4,6},{6,4},{8,10},{10,8},{12,14},{14,12},{1,3},{3,1},... | collective-permute-start | bytes 589832 | tf_op jit(solution)/shard_map/ppermute | solution.py:373
  50.5 13.6 %all-to-all-start = ((bf16[4,9,64,128]{3,2,1,0:T(8,128)(2,1)}), bf16[4,9,64,128]{3,2,1,0:T(8,128)(2,1)S(1)}, u32[]{:S(2)}, u32[]{:S(2)}) async-start(bf16[4,9,64,128]{3,2,1,0:T(8,128)(2,1)} %shard_map.63), calls=%async_computation | async-start | bytes 1179648 | tf_op jit(solution)/shard_map/all_to_all | solution.py:438
  54.0 20.0 %collective-permute-start.19 = (bf16[2,128,1024]{2,1,0:T(8,128)(2,1)}, bf16[2,128,1024]{2,1,0:T(8,128)(2,1)}, u32[]{:S(2)}, u32[]{:S(2)}) collective-permute-start(bf16[2,128,1024]{2,1,0:T(8,128)(2,1)} %copy-done.6), channel_id=1, source_target_pairs={{0,4},{2,6},{4,0},{6,2},{8,12},{10,14},{12,8},{14,10},{1,5},{3,7},... | collective-permute-start | bytes 1572872 | tf_op jit(solution)/shard_map/ppermute | solution.py:373
  55.5 20.8 %collective-permute-start.22 = (bf16[2,128,1024]{2,1,0:T(8,128)(2,1)}, bf16[2,128,1024]{2,1,0:T(8,128)(2,1)}, u32[]{:S(2)}, u32[]{:S(2)}) collective-permute-start(bf16[2,128,1024]{2,1,0:T(8,128)(2,1)} %copy-done.5), channel_id=1, source_target_pairs={{0,12},{2,14},{4,8},{6,10},{8,4},{10,6},{12,0},{14,2},{1,13},{3,15... | collective-permute-start | bytes 1572872 | tf_op jit(solution)/shard_map/ppermute | solution.py:373
  57.2 22.9 %collective-permute-start.21 = (bf16[2,128,1024]{2,1,0:T(8,128)(2,1)S(1)}, bf16[2,128,1024]{2,1,0:T(8,128)(2,1)}, u32[]{:S(2)}, u32[]{:S(2)}) collective-permute-start(bf16[2,128,1024]{2,1,0:T(8,128)(2,1)S(1)} %collective-permute-done.20.far_ref), channel_id=1, source_target_pairs={{2,14},{6,2},{10,6},{14,10},{3,15},{7,3},{11,7},{15,11},{18,30},{2... | collective-permute-start | bytes 1572872 | tf_op jit(solution)/shard_map/ppermute | solution.py:373
  64.7 11.8 %collective-permute-start.17 = (bf16[8,64,128]{2,1,0:T(8,128)(2,1)S(1)}, bf16[8,64,128]{2,1,0:T(8,128)(2,1)S(1)}, u32[]{:S(2)}, u32[]{:S(2)}) collective-permute-start(bf16[8,64,128]{2,1,0:T(8,128)(2,1)S(1)} %shard_map.64), channel_id=1, source_target_pairs={{0,112},{16,96},{32,80},{48,64},{64,48},{80,32},{96,16},{112,0},{1... | collective-permute-start | bytes 393224 | tf_op jit(solution)/shard_map/ppermute | solution.py:373
  68.2 10.7 %collective-permute-start.16 = (bf16[8,64,128]{2,1,0:T(8,128)(2,1)S(1)}, bf16[8,64,128]{2,1,0:T(8,128)(2,1)S(1)}, u32[]{:S(2)}, u32[]{:S(2)}) collective-permute-start(bf16[8,64,128]{2,1,0:T(8,128)(2,1)S(1)} %shard_map.64), channel_id=1, source_target_pairs={{0,96},{16,112},{32,64},{48,80},{64,32},{80,48},{96,0},{112,16},{1... | collective-permute-start | bytes 393224 | tf_op jit(solution)/shard_map/ppermute | solution.py:373
  74.0 9.5 %collective-permute-start.15 = (bf16[8,64,128]{2,1,0:T(8,128)(2,1)S(1)}, bf16[8,64,128]{2,1,0:T(8,128)(2,1)S(1)}, u32[]{:S(2)}, u32[]{:S(2)}) collective-permute-start(bf16[8,64,128]{2,1,0:T(8,128)(2,1)S(1)} %shard_map.64), channel_id=1, source_target_pairs={{0,80},{16,64},{32,112},{48,96},{64,16},{80,0},{96,48},{112,32},{1... | collective-permute-start | bytes 393224 | tf_op jit(solution)/shard_map/ppermute | solution.py:373
  76.2 7.3 %collective-permute-start.14 = (bf16[8,64,128]{2,1,0:T(8,128)(2,1)S(1)}, bf16[8,64,128]{2,1,0:T(8,128)(2,1)S(1)}, u32[]{:S(2)}, u32[]{:S(2)}) collective-permute-start(bf16[8,64,128]{2,1,0:T(8,128)(2,1)S(1)} %shard_map.64), channel_id=1, source_target_pairs={{0,64},{16,80},{32,96},{48,112},{64,0},{80,16},{96,32},{112,48},{1... | collective-permute-start | bytes 393224 | tf_op jit(solution)/shard_map/ppermute | solution.py:373
  76.5 7.1 %collective-permute-start.13 = (bf16[8,64,128]{2,1,0:T(8,128)(2,1)S(1)}, bf16[8,64,128]{2,1,0:T(8,128)(2,1)S(1)}, u32[]{:S(2)}, u32[]{:S(2)}) collective-permute-start(bf16[8,64,128]{2,1,0:T(8,128)(2,1)S(1)} %shard_map.64), channel_id=1, source_target_pairs={{0,48},{16,32},{32,16},{48,0},{64,112},{80,96},{96,80},{112,64},{1... | collective-permute-start | bytes 393224 | tf_op jit(solution)/shard_map/ppermute | solution.py:373
  79.0 5.7 %collective-permute-start.12 = (bf16[8,64,128]{2,1,0:T(8,128)(2,1)S(1)}, bf16[8,64,128]{2,1,0:T(8,128)(2,1)S(1)}, u32[]{:S(2)}, u32[]{:S(2)}) collective-permute-start(bf16[8,64,128]{2,1,0:T(8,128)(2,1)S(1)} %shard_map.64), channel_id=1, source_target_pairs={{0,32},{16,48},{32,0},{48,16},{64,96},{80,112},{96,64},{112,80},{1... | collective-permute-start | bytes 393224 | tf_op jit(solution)/shard_map/ppermute | solution.py:373
  80.1 4.5 %collective-permute-start.11 = (bf16[8,64,128]{2,1,0:T(8,128)(2,1)S(1)}, bf16[8,64,128]{2,1,0:T(8,128)(2,1)S(1)}, u32[]{:S(2)}, u32[]{:S(2)}) collective-permute-start(bf16[8,64,128]{2,1,0:T(8,128)(2,1)S(1)} %shard_map.64), channel_id=1, source_target_pairs={{0,16},{16,0},{32,48},{48,32},{64,80},{80,64},{96,112},{112,96},{1... | collective-permute-start | bytes 393224 | tf_op jit(solution)/shard_map/ppermute | solution.py:373
  85.4 5.2 %collective-permute-start.23 = (bf16[4,64,1024]{2,1,0:T(8,128)(2,1)S(1)}, bf16[4,64,1024]{2,1,0:T(8,128)(2,1)S(1)}, u32[]{:S(2)}, u32[]{:S(2)}) collective-permute-start(bf16[4,64,1024]{2,1,0:T(8,128)(2,1)S(1)} %shard_map.69), channel_id=1, source_target_pairs={{0,2},{2,0},{4,6},{6,4},{8,10},{10,8},{12,14},{14,12},{1,3},{3,1},... | collective-permute-start | bytes 1572872 | tf_op jit(solution)/shard_map/ppermute | solution.py:373
